TPU v7x, 128 devices: a whole 4x4x4 slice. The times are simulated.
128 devices in a mesh: row: 16 (over z_hi, y, core), col: 8 (over x, z_lo).
Axes of the slice: x: 4, y: 4, z: 4 (z_hi: 2, z_lo: 2; z = z_hi * 2 + z_lo), core: 2. Of those that a mesh axis runs over, the one named last changes fastest.
Arguments:
- tokens: bfloat16 [16384, 2048], P(('row', 'col')), may hold values from -30 to 30
- ln1_gain: float32 [2048], replicated, may hold values from 0.25 to 1.75
- qkv_weight: bfloat16 [2048, 16, 3, 128], P('row', 'col'), may hold values from -4 to 4
- out_weight: bfloat16 [2048, 2048], P('col', 'row'), may hold values from -0.125 to 0.125
- ln2_gain: float32 [2048], replicated, may hold values from 0.25 to 1.75
- ffn_in: bfloat16 [2048, 8192], P('row', 'col'), may hold values from -0.125 to 0.125
- ffn_out: bfloat16 [8192, 2048], P('col', 'row'), may hold values from -0.0625 to 0.0625
- expert_ids: int32 [16384, 1], P(('row', 'col')), may hold values from 0 to 63; in each aligned block of 128 rows (0 to 127, 128 to 255, ...) at most 4 rows name the same one
- expert_in: bfloat16 [128, 2048, 2048], P(('row', 'col')), may hold values from -0.125 to 0.125
- expert_out: bfloat16 [128, 2048, 2048], P(('row', 'col')), may hold values from -0.09375 to 0.09375
Outputs:
- block_out: bfloat16 [16384, 2048], P(('row', 'col'))
Inputs may be any that keep to these rules, and one draw needn't show every extreme that they name: `expert_ids`: among the tokens of one device no expert is named more than 4 times, and in every draw some expert is named exactly 4 times by the tokens of some device.
All inputs are finite; a program needn't handle non-finite values.
Results may differ from a plain program's by a relative error of at most 0.013.
Values may be sent and summed in bfloat16 or wider, within the bound.
A program may use at most 128 MiB of HBM per device.

v0:
```python
import heapq

import jax
import jax.numpy as jnp
from jax import lax
from jax.experimental import pallas as pl
from jax.experimental.pallas import tpu as pltpu
from jax.sharding import Mesh
from jax.sharding import PartitionSpec as P

ROW = ("zh", "y", "core")
COL = ("x", "zl")
ROW_COL = ("zh", "y", "core", "x", "zl")
BF16 = jnp.bfloat16
F32 = jnp.float32


class Spot:
    def __init__(self):
        self.x = lax.axis_index("x")
        self.y = lax.axis_index("y")
        self.zh = lax.axis_index("zh")
        self.zl = lax.axis_index("zl")
        self.core = lax.axis_index("core")
        self.row = (self.zh * 4 + self.y) * 2 + self.core
        z = self.zh * 2 + self.zl
        zp, zm = lax.rem(z + 1, 4), lax.rem(z + 3, 4)
        self.zhp, self.zhm = lax.div(zp, 2), lax.div(zm, 2)
        self.yp, self.ym = lax.rem(self.y + 1, 4), lax.rem(self.y + 3, 4)
        self.up = {
            "x": {"x": lax.rem(self.x + 1, 4)},
            "y": {"y": self.yp},
            "z": {"zh": self.zhp, "zl": lax.rem(zp, 2)},
        }
        self.down = {
            "x": {"x": lax.rem(self.x + 3, 4)},
            "y": {"y": self.ym},
            "z": {"zh": self.zhm, "zl": lax.rem(zm, 2)},
        }
        self.sibling = {"core": 1 - self.core}
        self.pair = {"zl": 1 - self.zl}


class Wire:
    def __init__(self, send_sems, recv_sems):
        self.send_sems, self.recv_sems = send_sems, recv_sems
        self.sent = []

    def send(self, src, dst, where):
        k = len(self.sent)
        copy = pltpu.make_async_remote_copy(
            src_ref=src,
            dst_ref=dst,
            send_sem=self.send_sems.at[k],
            recv_sem=self.recv_sems.at[k],
            device_id=where,
            device_id_type=pl.DeviceIdType.MESH,
        )
        copy.start()
        self.sent.append(copy)
        return copy


def greet(places):
    barrier = pltpu.get_barrier_semaphore()
    for place in places:
        pl.semaphore_signal(
            barrier, inc=1, device_id=place, device_id_type=pl.DeviceIdType.MESH
        )
    pl.semaphore_wait(barrier, len(places))


def run_streams(streams, late=()):
    queue, count = [], 0
    for stream in streams:
        step = next(stream, None)
        if step is not None:
            heapq.heappush(queue, (step[0], count, step[1], stream))
        count += 1
    while queue:
        _, n, copy, stream = heapq.heappop(queue)
        if copy is not None:
            copy.wait_recv()
        step = next(stream, None)
        if step is not None:
            heapq.heappush(queue, (step[0], n, step[1], stream))
        while late:
            step, stream = late.pop()
            heapq.heappush(queue, (step[0], count, step[1], stream))
            count += 1


def gather_weight(wire, at, own, local, whole, half, first, start, block):
    c, zh, y = at.core, at.zh, at.y
    rows = own.shape[0] // 2
    low, high = pl.ds(0, rows), pl.ds(rows, rows)
    if first == "y":
        a = wire.send(own, whole.at[0, zh, y, c, half], at.up["y"])
        b = wire.send(own, whole.at[0, zh, y, c, half], at.down["y"])
        yield start + 2 * block, a
        slot = whole.at[0, zh, at.ym, c, half, low]
        e = wire.send(slot, slot, at.up["y"])
        yield start + 2 * block, b
        slot = whole.at[0, zh, at.yp, c, half, high]
        f = wire.send(slot, slot, at.down["y"])
        yield start + 3 * block, e
        yield start + 3 * block, f
        local.wait()
        group = whole.at[0, zh, :, c, half]
        far = whole.at[1, zh, :, c, half]
        g = wire.send(group, far, at.up["z"])
        h = wire.send(group, far, at.down["z"])
        s = [wire.send(group, group, at.sibling)]
        yield start + 11 * block, g
        lower = pl.ds(0, 2)
        i = wire.send(
            whole.at[1, at.zhm, lower, c, half], whole.at[0, at.zhm, lower, c, half], at.up["z"]
        )
        s.append(wire.send(whole.at[1, at.zhm, :, c, half], whole.at[1, at.zhm, :, c, half], at.sibling))
        yield start + 11 * block, h
        upper = pl.ds(2, 2)
        j = wire.send(
            whole.at[1, at.zhp, upper, c, half], whole.at[0, at.zhp, upper, c, half], at.down["z"]
        )
        s.append(wire.send(whole.at[1, at.zhp, :, c, half], whole.at[1, at.zhp, :, c, half], at.sibling))
        yield start + 15 * block, i
        slot = whole.at[0, 1 - zh, lower, c, half]
        s.append(wire.send(slot, slot, at.sibling))
        yield start + 15 * block, j
        slot = whole.at[0, 1 - zh, upper, c, half]
        s.append(wire.send(slot, slot, at.sibling))
    else:
        a = wire.send(own, whole.at[1, zh, y, c, half], at.up["z"])
        b = wire.send(own, whole.at[1, zh, y, c, half], at.down["z"])
        yield start + 2 * block, a
        e = wire.send(
            whole.at[1, at.zhm, y, c, half, low], whole.at[0, at.zhm, y, c, half, low], at.up["z"]
        )
        yield start + 2 * block, b
        f = wire.send(
            whole.at[1, at.zhp, y, c, half, high], whole.at[0, at.zhp, y, c, half, high], at.down["z"]
        )
        yield start + 3 * block, e
        yield start + 3 * block, f
        local.wait()
        group = whole.at[:, :, y, c, half]
        g = wire.send(group, group, at.up["y"])
        h = wire.send(group, group, at.down["y"])
        s = [wire.send(group, group, at.sibling)]
        yield start + 11 * block, g
        slot = whole.at[0, :, at.ym, c, half]
        i = wire.send(slot, slot, at.up["y"])
        slot = whole.at[:, :, at.ym, c, half]
        s.append(wire.send(slot, slot, at.sibling))
        yield start + 11 * block, h
        slot = whole.at[1, :, at.yp, c, half]
        j = wire.send(slot, slot, at.down["y"])
        slot = whole.at[:, :, at.yp, c, half]
        s.append(wire.send(slot, slot, at.sibling))
        across = lax.rem(y + 2, 4)
        yield start + 15 * block, i
        slot = whole.at[0, :, across, c, half]
        s.append(wire.send(slot, slot, at.sibling))
        yield start + 15 * block, j
        slot = whole.at[1, :, across, c, half]
        s.append(wire.send(slot, slot, at.sibling))
    for n, copy in enumerate(s):
        yield start + 15 * block + 2 + n / 8, copy


def gather_x(wire, at, own, tiles, parts, start, block):
    half = own.shape[0] // 2 if parts == 2 else own.shape[0]
    low, high = pl.ds(0, half), pl.ds(half, half)
    if parts == 2:
        a1 = wire.send(own.at[low], tiles.at[3, low], at.up["x"])
        b1 = wire.send(own.at[high], tiles.at[1, high], at.down["x"])
        a2 = wire.send(own.at[high], tiles.at[3, high], at.up["x"])
        b2 = wire.send(own.at[low], tiles.at[1, low], at.down["x"])
        yield start + block, a1
        e = wire.send(tiles.at[3, low], tiles.at[2, low], at.up["x"])
        yield start + block, b1
        f = wire.send(tiles.at[1, high], tiles.at[2, high], at.down["x"])
        yield start + 2 * block, a2
        yield start + 2 * block, b2
        yield start + 3 * block, e
        yield start + 3 * block, f
    else:
        a = wire.send(own, tiles.at[3], at.up["x"])
        b = wire.send(own, tiles.at[1], at.down["x"])
        yield start + block, a
        e = wire.send(tiles.at[3], tiles.at[2], at.up["x"])
        yield start + block, b
        yield start + 2 * block, e


def scatter_x(wire, at, terms, got, passing, start, block):
    half = terms.shape[1] // 2
    low, high = pl.ds(0, half), pl.ds(half, half)
    c1 = wire.send(terms.at[2, low], passing.at[0], at.up["x"])
    c2 = wire.send(terms.at[2, high], passing.at[1], at.down["x"])
    a = wire.send(terms.at[1], got.at[0], at.up["x"])
    b = wire.send(terms.at[3], got.at[1], at.down["x"])
    yield start + block, c1
    d1 = wire.send(passing.at[0], got.at[2, low], at.up["x"])
    yield start + block, c2
    d2 = wire.send(passing.at[1], got.at[2, high], at.down["x"])
    yield start + 3 * block, a
    yield start + 3 * block, b
    yield start + 4 * block, d1
    yield start + 4 * block, d2


def comm_call(body, inputs, outs, scratch, copies, locals_, number, sent_bytes, name):
    return pl.pallas_call(
        body,
        out_shape=outs,
        in_specs=[pl.BlockSpec(memory_space=pl.ANY)] * len(inputs),
        out_specs=[pl.BlockSpec(memory_space=pl.ANY)] * len(outs),
        scratch_shapes=[
            *scratch,
            pltpu.SemaphoreType.DMA((copies,)),
            pltpu.SemaphoreType.DMA((copies,)),
            pltpu.SemaphoreType.DMA((max(1, locals_),)),
        ],
        compiler_params=pltpu.CompilerParams(
            collective_id=number, has_side_effects=True, vmem_limit_bytes=8 << 20
        ),
        name=name,
    )(*inputs)


def like(shape, dtype=BF16):
    return jax.ShapeDtypeStruct(shape, dtype)


GATHER_COPIES = 13


def first_gather(tokens, pos, qkv, out):
    def body(tok, pos_in, qkv_in, out_in, tiles, spots, qkv_all, out_all,
             tok_v, pos_v, qkv_v, out_v, ss, rs, ls):
        at = Spot()
        loads = [
            pltpu.make_async_copy(tok, tok_v, ls.at[0]),
            pltpu.make_async_copy(pos_in, pos_v, ls.at[1]),
            pltpu.make_async_copy(qkv_in, qkv_v, ls.at[2]),
            pltpu.make_async_copy(out_in, out_v, ls.at[3]),
        ]
        for load in loads:
            load.start()
        greet([at.up["x"], at.down["x"], at.up["y"], at.down["y"], at.up["z"], at.down["z"], at.sibling])
        for load in loads:
            load.wait()
        stores = [
            pltpu.make_async_copy(tok_v, tiles.at[0], ls.at[4]),
            pltpu.make_async_copy(pos_v, spots.at[0], ls.at[5]),
            *[
                pltpu.make_async_copy(src.at[h], dst.at[0, at.zh, at.y, at.core, h], ls.at[6 + 2 * n + h])
                for n, (src, dst) in enumerate(((qkv_v, qkv_all), (out_v, out_all)))
                for h in range(2)
            ],
        ]
        for store in stores:
            store.start()
        wire = Wire(ss, rs)
        run_streams([
            gather_x(wire, at, pos_v, spots, 1, 0, 2),
            gather_x(wire, at, tok_v, tiles, 2, 0, 5.7),
            gather_weight(wire, at, qkv_v.at[0], stores[2], qkv_all, 0, "y", 0, 1.1),
            gather_weight(wire, at, qkv_v.at[1], stores[3], qkv_all, 1, "z", 0, 1.1),
            gather_weight(wire, at, out_v.at[0], stores[4], out_all, 0, "y", 1, 1.4),
            gather_weight(wire, at, out_v.at[1], stores[5], out_all, 1, "z", 1, 1.4),
        ])
        for store in stores[:2]:
            store.wait()
        for copy in wire.sent:
            copy.wait_send()

    outs = [
        like((4, *tokens.shape)),
        like((4, *pos.shape), jnp.int32),
        like((2, 2, 4, 2, *qkv.shape)),
        like((2, 2, 4, 2, *out.shape)),
    ]
    scratch = [
        pltpu.VMEM(tokens.shape, BF16),
        pltpu.VMEM(pos.shape, jnp.int32),
        pltpu.VMEM(qkv.shape, BF16),
        pltpu.VMEM(out.shape, BF16),
    ]
    return comm_call(body, [tokens, pos, qkv, out], outs, scratch,
                     9 + 4 * GATHER_COPIES, 10, 1, 0, "gather_first")


def pair_swap(mine, number, name):
    def body(src, dst, ss, rs, ls):
        at = Spot()
        greet([at.pair])
        wire = Wire(ss, rs)
        copy = wire.send(src.at[1], dst, at.pair)
        copy.wait()

    return comm_call(body, [mine], [like(mine.shape[1:])], [], 1, 0, number, 0, name)[0]


def scatter_and_weight(terms, weight, number, name):
    def body(src, w_in, got, passing, w_all, w_v, ss, rs, ls):
        at = Spot()
        load = pltpu.make_async_copy(w_in, w_v, ls.at[0])
        load.start()
        greet([at.up["x"], at.down["x"], at.up["y"], at.down["y"], at.up["z"], at.down["z"], at.sibling])
        load.wait()
        stores = [
            pltpu.make_async_copy(w_v.at[h], w_all.at[0, at.zh, at.y, at.core, h], ls.at[1 + h])
            for h in range(2)
        ]
        for store in stores:
            store.start()
        wire = Wire(ss, rs)
        run_streams([
            scatter_x(wire, at, src, got, passing, 0, 5.7),
            gather_weight(wire, at, w_v.at[0], stores[0], w_all, 0, "y", 0, 1.4),
            gather_weight(wire, at, w_v.at[1], stores[1], w_all, 1, "z", 0, 1.4),
        ])
        for copy in wire.sent:
            copy.wait_send()

    rows, width = terms.shape[1:]
    outs = [
        like((3, rows, width)),
        like((2, rows // 2, width)),
        like((2, 2, 4, 2, *weight.shape)),
    ]
    got, _, whole = comm_call(body, [terms, weight], outs, [pltpu.VMEM(weight.shape, BF16)],
                              6 + 2 * GATHER_COPIES, 3, number, 0, name)
    return got, whole


def gather_and_weight(block, weight, number, name):
    def body(src, w_in, tiles, w_all, src_v, w_v, ss, rs, ls):
        at = Spot()
        loads = [
            pltpu.make_async_copy(src, src_v, ls.at[0]),
            pltpu.make_async_copy(w_in, w_v, ls.at[1]),
        ]
        for load in loads:
            load.start()
        greet([at.up["x"], at.down["x"], at.up["y"], at.down["y"], at.up["z"], at.down["z"], at.sibling])
        for load in loads:
            load.wait()
        stores = [pltpu.make_async_copy(src_v, tiles.at[0], ls.at[2])] + [
            pltpu.make_async_copy(w_v.at[h], w_all.at[0, at.zh, at.y, at.core, h], ls.at[3 + h])
            for h in range(2)
        ]
        for store in stores:
            store.start()
        wire = Wire(ss, rs)
        run_streams([
            gather_x(wire, at, src_v, tiles, 2, 0, 5.7),
            gather_weight(wire, at, w_v.at[0], stores[1], w_all, 0, "y", 0, 1.4),
            gather_weight(wire, at, w_v.at[1], stores[2], w_all, 1, "z", 0, 1.4),
        ])
        stores[0].wait()
        for copy in wire.sent:
            copy.wait_send()

    outs = [like((4, *block.shape)), like((2, 2, 4, 2, *weight.shape))]
    scratch = [pltpu.VMEM(block.shape, BF16), pltpu.VMEM(weight.shape, BF16)]
    return comm_call(body, [block, weight], outs, scratch,
                     6 + 2 * GATHER_COPIES, 5, number, 0, name)


def layer_norm(row_data, gain_vector):
    row_data = row_data.astype(F32)
    centered = row_data - jnp.mean(row_data, axis=-1, keepdims=True)
    spread = jnp.mean(centered * centered, axis=-1, keepdims=True)
    return centered * lax.rsqrt(spread + 1e-06) * gain_vector


def gelu(v):
    return v * (0.5 + 0.5 * lax.erf(v * 0.5**0.5))


def dot(a, b):
    return jnp.dot(a, b, preferred_element_type=F32)


def dot_nt(a, b):
    return lax.dot_general(a, b, (((1,), (1,)), ((), ())), preferred_element_type=F32)


def tail_kernel(table, normed, hidden, placed, in_all, down_all, expert_in, expert_out, number):
    width = normed.shape[1]
    chunk, chunks = 512, width // 512

    def body(tab, nor, hid, pla, win, wdown, ein, eout, out,
             nor_v, hid_v, pla_v, win_v, wdown_v, ein_v, eout_v,
             units, dense, xx, aside, passing, away, mine, hop, near, ahead, sib,
             terms, got, across, ss, rs, ls):
        at = Spot()
        cross = {"zh": 1 - at.zh, "zl": 1 - at.zl}
        own_load = pltpu.make_async_copy(tab.at[:, 0, 0], xx.at[pl.ds(0, 2), 0, 0], ls.at[0])
        pairs = [(nor, nor_v), (win, win_v), (wdown, wdown_v), (ein, ein_v), (eout, eout_v), (pla, pla_v), (hid, hid_v)]
        loads = [pltpu.make_async_copy(src, dst, ls.at[1 + n]) for n, (src, dst) in enumerate(pairs)]
        own_load.start()
        for load in loads:
            load.start()
        greet([at.up["x"], at.down["x"], at.up["y"], at.down["y"], at.sibling, at.pair, cross])
        wire = Wire(ss, rs)
        both = pl.ds(0, 2)
        core0 = wire.send(tab.at[:, 0, 1], xx.at[both, 0, 1], at.sibling)
        core1 = wire.send(tab.at[:, pl.ds(1, 3), 1], aside, at.sibling)
        pair_in, far_in = [], []

        def z_part(src, where, t):
            pair_in.append(wire.send(src(1), xx.at[(2, *where)], at.pair))
            x = wire.send(src(0), xx.at[(3, *where)], cross)
            yield t, x
            far_in.append(wire.send(xx.at[(3, *where)], xx.at[(4, *where)], at.pair))

        def held(where):
            return lambda n: xx.at[(n, *where)]

        def own_y():
            yield from z_part(lambda n: tab.at[n, 0, 0], (0, 0), 2.5)

        def sib_y():
            yield 1.5, core0
            yield from z_part(held((0, 1)), (0, 1), 5)

        y1 = wire.send(tab.at[:, 1, 0], xx.at[both, 1, 0], at.up["y"])
        y3 = wire.send(tab.at[:, 3, 0], xx.at[both, 3, 0], at.down["y"])
        y2 = wire.send(tab.at[:, 2, 0], passing.at[0], at.up["y"])
        second = {}

        def middle():
            yield 1.6, core1
            second[2] = wire.send(aside.at[:, 1], passing.at[1], at.down["y"])
            second[1] = wire.send(aside.at[:, 0], xx.at[both, 1, 1], at.up["y"])
            second[3] = wire.send(aside.at[:, 2], xx.at[both, 3, 1], at.down["y"])
            yield 6, y2
            e = wire.send(passing.at[0], xx.at[both, 2, 0], at.up["y"])
            yield 6.2, second[2]
            f = wire.send(passing.at[1], xx.at[both, 2, 1], at.down["y"])
            yield 8, y1
            yield 9, second[1]
            later.append(z_part(held((1,)), (1,), 15))
            yield from start_later()
            yield 9, y3
            yield 9.5, second[3]
            later.append(z_part(held((3,)), (3,), 18))
            yield from start_later()
            yield 12, e
            yield 12, f
            later.append(z_part(held((2,)), (2,), 21))
            yield from start_later()

        later = []
        running = []

        def start_later():
            stream = later.pop()
            step = next(stream)
            running.append((step, stream))
            return
            yield

        tile = 256

        def ffn():
            t = 3.0
            yield t, None
            loads[0].wait()
            loads[1].wait()
            for part in range(4):
                yield t, None
                t += 1.6

                def step(n, carry, part=part):
                    columns = pl.ds(pl.multiple_of(part * 512 + n * tile, tile), tile)
                    source = pl.ds(pl.multiple_of((part % 2) * 512 + n * tile, tile), tile)
                    inner = dot(nor_v[...], win_v[part // 2, :, source])
                    units[:, columns] = gelu(inner).astype(BF16)
                    return carry

                lax.fori_loop(0, 2, step, 0)
            loads[2].wait()
            for part in range(4):
                yield t, None
                t += 1.6

                def step(n, carry, part=part):
                    columns = pl.ds(pl.multiple_of(part * 512 + n * tile, tile), tile)
                    dense[:, columns] = dot_nt(units[:, pl.ds(0, 1024)], wdown_v[0, columns, :]) + dot_nt(
                        units[:, pl.ds(1024, 1024)], wdown_v[1, columns, :]
                    )
                    return carry

                lax.fori_loop(0, 2, step, 0)

        queue = [own_y(), sib_y(), middle(), ffn()]
        run_streams(queue, running)
        own_load.wait()
        for copy in pair_in:
            copy.wait_recv()
        loads[3].wait()

        def expert_up(first):
            def step(n, carry):
                columns = pl.ds(pl.multiple_of(n * tile, tile), tile)
                rows = xx[pl.ds(1 + first, 2)].reshape(256, width)
                inner = dot(rows, ein_v[:, columns])
                units[pl.ds(first * 128, 256), columns] = gelu(inner).astype(BF16)
                return carry

            lax.fori_loop(0, width // tile, step, 0)

        expert_up(0)
        for copy in far_in:
            copy.wait_recv()
        expert_up(2)
        loads[4].wait()
        loads[5].wait()
        loads[6].wait()

        def one_chunk(j):
            yield 1.5 * j, None
            for n in range(chunk // tile):
                inside = pl.ds(n * tile, tile)
                part = dot(units[...], eout_v[:, pl.ds(j * chunk + n * tile, tile)]).astype(BF16)
                part = part.reshape(4, 4, 2, 16, tile)
                mine[j, 0, :, :, :, inside] = part[0]
                away[j, :, :, :, :, inside] = part[1:]
            z1 = wire.send(away.at[j, 0], mine.at[j, 1], at.pair)
            z3 = wire.send(away.at[j, 2], hop.at[j], at.pair)
            z2 = wire.send(away.at[j, 1], mine.at[j, 2], cross)
            t = 5.6 * j
            yield t + 7, z3
            f = wire.send(hop.at[j], mine.at[j, 3], cross)
            yield t + 7, z1
            yield t + 7, z2
            yield t + 10, f
            c = wire.send(mine.at[j, :, 2, 0], near.at[j, 0], at.down["y"])
            d = wire.send(mine.at[j, :, 2, 1], near.at[j, 1], at.up["y"])
            a = wire.send(mine.at[j, :, 1], ahead.at[j, :, 1], at.down["y"])
            b = wire.send(mine.at[j, :, 3], ahead.at[j, :, 3], at.up["y"])
            k0 = wire.send(mine.at[j, :, 0, 1], sib.at[j, :, 0], at.sibling)
            yield t + 13, c
            c2 = wire.send(near.at[j, 0], ahead.at[j, :, 2, 0], at.down["y"])
            yield t + 13, d
            d2 = wire.send(near.at[j, 1], ahead.at[j, :, 2, 1], at.up["y"])
            yield t + 16, a
            yield t + 16, b
            yield t + 17, c2
            yield t + 17, d2
            k1 = wire.send(ahead.at[j, :, pl.ds(1, 3), 1], sib.at[j, :, pl.ds(1, 3)], at.sibling)
            yield t + 18.5, k0
            yield t + 18.5, k1
            columns = pl.ds(j * chunk, chunk)
            first = jnp.concatenate(
                [mine[j, :, pl.ds(0, 1), 0], ahead[j, :, pl.ds(1, 3), 0]], axis=1
            ).reshape(256, chunk)
            total = dense[:, columns] + dot(pla_v[:, pl.ds(0, 256)], first)
            total = total + dot(pla_v[:, pl.ds(256, 256)], sib[j].reshape(256, chunk))
            terms[j] = total.astype(BF16).reshape(4, 128, chunk)
            yield from scatter_x(wire, at, terms.at[j], got.at[j], across.at[j], t + 19, 1.6)
            total = hid_v[:, columns].astype(F32) + terms[j, 0].astype(F32)
            for n in range(3):
                total = total + got[j, n].astype(F32)
            out[:, columns] = total.astype(BF16)

        run_streams([one_chunk(j) for j in range(chunks)])
        for copy in wire.sent:
            copy.wait_send()

    inputs = [table, normed, hidden, placed, in_all, down_all, expert_in, expert_out]
    copies = 25 + chunks * 18
    return pl.pallas_call(
        body,
        out_shape=like((128, width)),
        in_specs=[pl.BlockSpec(memory_space=pl.ANY)] * len(inputs),
        out_specs=pl.BlockSpec(memory_space=pltpu.VMEM),
        scratch_shapes=[
            *[pltpu.VMEM(a.shape, BF16) for a in (normed, hidden, placed, in_all, down_all, expert_in, expert_out)],
            pltpu.VMEM((512, width), BF16),
            pltpu.VMEM((512, width), F32),
            pltpu.VMEM((5, 4, 2, 16, width), BF16),
            pltpu.VMEM((2, 3, 16, width), BF16),
            pltpu.VMEM((2, 2, 16, width), BF16),
            pltpu.VMEM((chunks, 3, 4, 2, 16, chunk), BF16),
            pltpu.VMEM((chunks, 4, 4, 2, 16, chunk), BF16),
            pltpu.VMEM((chunks, 4, 2, 16, chunk), BF16),
            pltpu.VMEM((chunks, 2, 4, 16, chunk), BF16),
            pltpu.VMEM((chunks, 4, 4, 2, 16, chunk), BF16),
            pltpu.VMEM((chunks, 4, 4, 16, chunk), BF16),
            pltpu.VMEM((chunks, 4, 128, chunk), BF16),
            pltpu.VMEM((chunks, 3, 128, chunk), BF16),
            pltpu.VMEM((chunks, 2, 64, chunk), BF16),
            pltpu.SemaphoreType.DMA((copies,)),
            pltpu.SemaphoreType.DMA((copies,)),
            pltpu.SemaphoreType.DMA((8,)),
        ],
        compiler_params=pltpu.CompilerParams(
            collective_id=number, has_side_effects=True, vmem_limit_bytes=67_000_000
        ),
        name="experts_and_dense",
    )(*inputs)


def shards(
    tokens, ln1_gain, qkv_weight, out_weight, ln2_gain, ffn_in, ffn_out,
    expert_ids, expert_in, expert_out,
):
    count, width = tokens.shape
    experts, slots = 64, 4
    chosen = expert_ids[:, 0]
    one_hot = (chosen[:, None] == jnp.arange(experts, dtype=jnp.int32)[None, :]).astype(BF16)
    order = jnp.arange(count, dtype=jnp.int32)
    before = (order[None, :] < order[:, None]).astype(BF16)
    earlier = jnp.sum(dot(before, one_hot) * one_hot.astype(F32), axis=1)
    pos = (chosen * slots + earlier.astype(jnp.int32))[None, :]

    heads, head_dim = qkv_weight.shape[1], qkv_weight.shape[3]
    qkv_width = heads * 3 * head_dim
    tiles, spots, qkv_all, out_all = first_gather(
        tokens, pos, qkv_weight.reshape(2, -1, qkv_width), out_weight.T.reshape(2, -1, out_weight.shape[0])
    )
    normed = layer_norm(tiles.reshape(4 * count, width), ln1_gain).astype(BF16)
    qkv_all = qkv_all.reshape(2, width, qkv_width)
    projected = jnp.stack([dot(normed, qkv_all[n]).astype(BF16) for n in range(2)])
    other = pair_swap(projected, 2, "swap_heads")
    image = jnp.concatenate([projected[0], other]).reshape(-1, heads, 3, head_dim)
    scores = jnp.einsum(
        "qhd,khd->hqk", image[:, :, 0], image[:, :, 1], preferred_element_type=F32
    ) * head_dim ** (-0.5)
    weights = jnp.exp(scores - jnp.max(scores, axis=-1, keepdims=True))
    probabilities = (weights / jnp.sum(weights, axis=-1, keepdims=True)).astype(BF16)
    attended = jnp.einsum("hqk,khd->qhd", probabilities, image[:, :, 2], preferred_element_type=F32)
    attended = attended.astype(BF16).reshape(2, 4 * count, heads * head_dim)
    other = pair_swap(attended, 3, "swap_attended")
    out_all = out_all.reshape(2, width, -1)
    mixed = dot_nt(attended[0], out_all[0]) + dot_nt(other, out_all[1])
    mixed = mixed.astype(BF16).reshape(4, count, width)
    got, in_all = scatter_and_weight(mixed, ffn_in.reshape(2, -1, ffn_in.shape[1]), 4, "scatter_heads")
    hidden = (
        tokens.astype(F32) + mixed[0].astype(F32) + got[0].astype(F32) + got[1].astype(F32) + got[2].astype(F32)
    ).astype(BF16)
    normed_mine = layer_norm(hidden, ln2_gain).astype(BF16)
    down = ffn_out.T
    tiles, down_all = gather_and_weight(normed_mine, down.reshape(2, -1, down.shape[1]), 5, "gather_normed")
    normed = tiles.reshape(4 * count, width)

    zh, y, core, x = (lax.axis_index(name) for name in ("zh", "y", "core", "x"))

    def named(pair, dy, dc):
        expert = (((jnp.where(pair, zh, 1 - zh) * 4 + (y + dy) % 4) * 2 + (core + dc) % 2) * 4) + x
        wanted = expert[..., None] * slots + jnp.arange(slots, dtype=jnp.int32)
        hit = wanted[..., None, :, None, None] == spots.reshape(4, count)
        same = jnp.arange(4)[:, None, None, None] == jnp.arange(4)[None, None, :, None]
        return (hit & same).astype(BF16).reshape(-1, 4 * count)

    def steps(size, dim, dims):
        return lax.broadcasted_iota(jnp.int32, dims, dim)

    dims = (2, 4, 2)
    sending = named(steps(2, 0, dims) == 1, steps(4, 1, dims), steps(2, 2, dims))
    table = dot(sending, normed).astype(BF16).reshape(2, 4, 2, 16, width)
    dims = (2, 4, 4)
    placed = named(steps(4, 1, dims) < 2, steps(4, 2, dims), steps(2, 0, dims)).T
    return tail_kernel(
        table, normed, hidden, placed, in_all.reshape(2, width, -1), down_all.reshape(2, width, -1),
        expert_in[0], expert_out[0], 6,
    )


def solution(mesh):
    split = Mesh(mesh.devices.reshape(2, 4, 2, 4, 2), ROW_COL)
    in_specs = (
        P(ROW_COL, None),
        P(),
        P(ROW, COL, None, None),
        P(COL, ROW),
        P(),
        P(ROW, COL),
        P(COL, ROW),
        P(ROW_COL, None),
        P(ROW_COL, None, None),
        P(ROW_COL, None, None),
    )
    out_specs = P(ROW_COL, None)
    return jax.shard_map(shards, mesh=split, in_specs=in_specs, out_specs=out_specs, check_vma=False)
```

profile of v0, /device:TPU:1, one launch (start us, length us, event | category | flops | bytes accessed | tf_op | source)
XLA Modules:
  0.0 277.0 jit_solution(18130997045585711909)
XLA Ops:
  0.0 0.9 fusion.16
  0.9 0.7 bitcast_add_fusion.pos_in
  1.7 0.1 add_multiply_fusion.1
  1.7 0.1 add_multiply_fusion
  2.0 0.9 copy.21
  2.9 1.0 copy.20
  4.0 0.2 reshape.219.qkv_in
  4.1 1.1 copy.28
  5.2 1.0 copy-done.4
  6.3 37.7 %gather_first.1 = (bf16[4,128,2048]{2,1,0:T(8,128)(2,1)S(1)}, s32[4,1,128]{2,1,0:T(1,128)S(1)}, bf16[2,2,4,2,2,64,768]{6,5,4,3,2,1,0:T(8,128)(2,1)S(1)}, bf16[2,2,4,2,2,64,256]{6,5,4,3,2,1,0:T(8,128)(2,1)S(1)}) custom-call(bf16[128,2048]{1,0:T(8,128)(2,1)S(1)} %copy-done.4, s32[1,128]{1,0:T(1,128)S(1)} %bitcast_add_fusion.pos_in, ...), custom_call_target="tpu_custom_call" | custom-call | tf_op jit(solution)/shard_map/gather_first/pallas_call | solution.py:214
  44.0 2.6 copy-done.3
  46.7 0.3 convert_reduce_fusion
  47.0 0.7 fusion.6
  47.7 2.0 fusion.8
  49.8 0.1 broadcast_compare_fusion.1
  49.9 0.2 broadcast_compare_fusion
  50.1 0.2 broadcast_and_fusion
  50.3 0.4 and_convert_fusion
  50.7 0.1 copy.42
  50.7 1.0 copy.29
  51.8 1.2 fusion.35
  52.9 3.4 %fusion.34 = (bf16[1,2,4,2,2,64,768]{6,5,4,3,2,1,0:T(8,128)(2,1)S(1)}, bf16[1,2,4,2,2,64,768]{6,5,4,3,2,1,0:T(8,128)(2,1)S(1)}) fusion(bf16[2,2,4,2,2,64,768]{6,5,4,3,2,1,0:T(8,128)(2,1)} %copy-done.3), kind=kLoop, calls=%fused_computation.77 | loop fusion | bytes 12582912 | tf_op jit(solution)/shard_map/slice | solution.py:630
  56.4 1.8 convolution_convert_fusion.2
  58.2 1.8 fusion.12
  60.0 0.1 pad_maximum_fusion.src
  60.1 18.8 %swap_heads.1 = bf16[512,768]{1,0:T(8,128)(2,1)S(1)} custom-call(bf16[2,512,768]{2,1,0:T(8,128)(2,1)S(1)} %pad_maximum_fusion.src), custom_call_target="tpu_custom_call" | custom-call | tf_op jit(solution)/shard_map/swap_heads/pallas_call | solution.py:214
  78.9 0.1 pad_maximum_fusion.1
  79.1 1.7 copy.22
  80.7 7.2 %fusion.36 = (f32[2,1024]{1,0:T(2,128)S(1)}, f32[2,1024,1024]{1,2,0:T(8,128)}) fusion(bf16[1024,2,3,128]{0,3,2,1:T(8,128)(2,1)} %bitcast.117), kind=kOutput, calls=%fused_computation.79 | convolution fusion | flops 543163392 | bytes 9445376 | tf_op jit(solution)/shard_map/sub | solution.py:636
  87.9 4.3 %fusion.15 = bf16[1024,2,128]{0,2,1:T(8,128)(2,1)S(1)} fusion(f32[2,1024,1024]{1,2,0:T(8,128)} %get-tuple-element.28, f32[2,1024]{1,0:T(2,128)S(1)} %get-tuple-element.27, bf16[1024,2,3,128]{0,3,2,1:T(8,128)(2,1)} %bitcast.118), kind=kOutput, calls=%fused_computation.26 | convolution fusion | flops 541327360 | bytes 9445376 | tf_op jit(solution)/shard_map/hqk,khd->qhd/dot_general | solution.py:638
  92.3 1.2 reshape.234
  93.5 1.5 copy.31.src
  94.9 6.7 %swap_attended.1 = bf16[512,256]{1,0:T(8,128)(2,1)S(1)} custom-call(bf16[2,512,256]{2,1,0:T(8,128)(2,1)S(1)} %copy.31.src), custom_call_target="tpu_custom_call" | custom-call | tf_op jit(solution)/shard_map/swap_attended/pallas_call | solution.py:214
  101.7 0.8 fusion.37
  102.4 0.8 add_convert_fusion
  103.2 0.2 copy-done.6
  103.4 35.0 %scatter_heads.1 = (bf16[3,128,2048]{2,1,0:T(8,128)(2,1)S(1)}, bf16[2,64,2048]{2,1,0:T(8,128)(2,1)}, bf16[2,2,4,2,2,64,1024]{6,5,4,3,2,1,0:T(8,128)(2,1)S(1)}) custom-call(bf16[4,128,2048]{2,1,0:T(8,128)(2,1)S(1)} %bitcast.93, bf16[2,64,1024]{2,1,0:T(8,128)(2,1)S(1)} %bitcast.99), custom_call_target="tpu_custom_call" | custom-call | tf_op jit(solution)/shard_map/scatter_heads/pallas_call | solution.py:214
  138.4 3.2 %copy-done.1 = bf16[2,2,4,2,2,64,1024]{6,5,4,3,2,1,0:T(8,128)(2,1)} copy-done((bf16[2,2,4,2,2,64,1024]{6,5,4,3,2,1,0:T(8,128)(2,1)}, bf16[2,2,4,2,2,64,1024]{6,5,4,3,2,1,0:T(8,128)(2,1)S(1)}, u32[]{:S(2)}) %copy-start.1) | copy-done | bytes 8388632
  141.6 0.5 convert_reduce_fusion.1
  142.2 0.3 fusion.17
  142.5 0.5 copy-done.7
  142.9 0.4 fusion.19.src
  143.3 33.1 %gather_normed.1 = (bf16[4,128,2048]{2,1,0:T(8,128)(2,1)S(1)}, bf16[2,2,4,2,2,64,1024]{6,5,4,3,2,1,0:T(8,128)(2,1)S(1)}) custom-call(bf16[128,2048]{1,0:T(8,128)(2,1)S(1)} %fusion.19.src, bf16[2,64,1024]{2,1,0:T(8,128)(2,1)S(1)} %bitcast.98), custom_call_target="tpu_custom_call" | custom-call | tf_op jit(solution)/shard_map/gather_normed/pallas_call | solution.py:214
  176.4 3.2 %copy-done.2 = bf16[2,2,4,2,2,64,1024]{6,5,4,3,2,1,0:T(8,128)(2,1)} copy-done((bf16[2,2,4,2,2,64,1024]{6,5,4,3,2,1,0:T(8,128)(2,1)}, bf16[2,2,4,2,2,64,1024]{6,5,4,3,2,1,0:T(8,128)(2,1)S(1)}, u32[]{:S(2)}) %copy-start.2) | copy-done | bytes 8388632
  179.6 1.3 copy-done
  181.0 1.7 convolution_convert_fusion
  182.7 92.4 %experts_and_dense.1 = bf16[128,2048]{1,0:T(8,128)(2,1)} custom-call(bf16[2,4,2,16,2048]{4,3,2,1,0:T(8,128)(2,1)} %bitcast.105, bf16[512,2048]{1,0:T(8,128)(2,1)} %bitcast.95, bf16[128,2048]{1,0:T(8,128)(2,1)} %copy-done.7, bf16[512,512]{1,0:T(8,128)(2,1)} %bitcast.111, bf16[2,2048,1024]{2,1,0:T(8,128)(2,1)} %bitcast.96, bf16[2,2048,1024]{2,1,0:T(8,128)(2,1)} %bitcast.97, ...), custom_call_target="tpu_custom_call" | custom-call | tf_op jit(solution)/shard_map/experts_and_dense/pallas_call | solution.py:578
  275.1 1.9 copy.44
  (31 shorter events, 0.3 us)
Async XLA Ops:
  2.9 44.8 %copy-start.10 = (f32[2048]{0:T(1024)S(1)}, f32[2048]{0:T(1024)}, u32[]{:S(2)}) copy-start(f32[2048]{0:T(1024)} %param.11) | copy-start | bytes 24580
  5.2 1.0 copy-start.4
  44.0 2.7 copy-start.3
  52.9 3.4 %copy-start.9 = (bf16[4,128,2048]{2,1,0:T(8,128)(2,1)S(1)}, bf16[4,128,2048]{2,1,0:T(8,128)(2,1)}, u32[]{:S(2)}) copy-start(bf16[4,128,2048]{2,1,0:T(8,128)(2,1)} %fusion.8) | copy-start | bytes 6291460
  92.2 9.4 %copy-start.8 = (bf16[1,2,4,2,2,64,256]{6,5,4,3,2,1,0:T(8,128)(2,1)S(1)}, bf16[1,2,4,2,2,64,256]{6,5,4,3,2,1,0:T(8,128)(2,1)}, u32[]{:S(2)}) copy-start(bf16[1,2,4,2,2,64,256]{6,5,4,3,2,1,0:T(8,128)(2,1)} %get-tuple-element.26) | copy-start | bytes 3145732
  102.4 1.0 copy-start.6
  102.4 39.2 %copy-start.5 = (bf16[128,2048]{1,0:T(8,128)(2,1)S(1)}, bf16[128,2048]{1,0:T(8,128)(2,1)}, u32[]{:S(2)}) copy-start(bf16[128,2048]{1,0:T(8,128)(2,1)} %tok.1) | copy-start | bytes 1572868
  103.2 39.7 %copy-start.11 = (f32[2048]{0:T(1024)S(1)}, f32[2048]{0:T(1024)}, u32[]{:S(2)}) copy-start(f32[2048]{0:T(1024)} %param.14) | copy-start | bytes 24580
  138.4 3.2 %copy-start.1 = (bf16[2,2,4,2,2,64,1024]{6,5,4,3,2,1,0:T(8,128)(2,1)}, bf16[2,2,4,2,2,64,1024]{6,5,4,3,2,1,0:T(8,128)(2,1)S(1)}, u32[]{:S(2)}) copy-start(bf16[2,2,4,2,2,64,1024]{6,5,4,3,2,1,0:T(8,128)(2,1)S(1)} %get-tuple-element.19) | copy-start | bytes 25165828
  142.1 0.8 copy-start.7
  176.4 3.2 %copy-start.2 = (bf16[2,2,4,2,2,64,1024]{6,5,4,3,2,1,0:T(8,128)(2,1)}, bf16[2,2,4,2,2,64,1024]{6,5,4,3,2,1,0:T(8,128)(2,1)S(1)}, u32[]{:S(2)}) copy-start(bf16[2,2,4,2,2,64,1024]{6,5,4,3,2,1,0:T(8,128)(2,1)S(1)} %get-tuple-element.20) | copy-start | bytes 25165828
  179.6 1.3 copy-start
where the time goes:
time: 277 us
  Pallas kernels  224 us (81%)
  local copies, waits for them, and re-layouts  27.3 us (10%)
  matrix products  19.2 us (7%)
  other arithmetic  6.46 us (2%)
    pallas_call x5, Pallas kernels, comm_call(): pl.pallas_call(body, out_shape=outs, in_specs=[pl.BlockSpec(memory_space=...  131 us
    pallas_call x1, Pallas kernels, tail_kernel(): pl.pallas_call(body, out_shape=like((128, width)), in_specs=[pl.BlockSpec...  92.4 us
    unnamed x27, local copies, waits for them, and re-layouts  15.1 us
    sub x1, matrix products, shards(): weights = jnp.exp(scores - jnp.max(scores, axis=-1, keepdims=True))  7.2 us
    dot_general x4, matrix products, dot(): return jnp.dot(a, b, preferred_element_type=F32)  6.19 us

commit v1 on v0

--- a/solution.py
+++ b/solution.py
@@ -90,7 +90,7 @@
             count += 1
 
 
-def gather_weight(wire, at, own, local, whole, half, first, start, block):
+def gather_weight(wire, at, own, local, whole, half, first, start, block, hold=None):
     c, zh, y = at.core, at.zh, at.y
     rows = own.shape[0] // 2
     low, high = pl.ds(0, rows), pl.ds(rows, rows)
@@ -105,7 +105,11 @@
         f = wire.send(slot, slot, at.down["y"])
         yield start + 3 * block, e
         yield start + 3 * block, f
-        local.wait()
+        if local is not None:
+            local.wait()
+        if hold is not None:
+            yield hold, None
+            start = hold
         group = whole.at[0, zh, :, c, half]
         far = whole.at[1, zh, :, c, half]
         g = wire.send(group, far, at.up["z"])
@@ -142,7 +146,11 @@
         )
         yield start + 3 * block, e
         yield start + 3 * block, f
-        local.wait()
+        if local is not None:
+            local.wait()
+        if hold is not None:
+            yield hold, None
+            start = hold
         group = whole.at[:, :, y, c, half]
         g = wire.send(group, group, at.up["y"])
         h = wire.send(group, group, at.down["y"])
@@ -168,7 +176,7 @@
         yield start + 15 * block + 2 + n / 8, copy
 
 
-def gather_x(wire, at, own, tiles, parts, start, block):
+def gather_x(wire, at, own, tiles, parts, start, block, ready=lambda s: None):
     half = own.shape[0] // 2 if parts == 2 else own.shape[0]
     low, high = pl.ds(0, half), pl.ds(half, half)
     if parts == 2:
@@ -181,9 +189,12 @@
         yield start + block, b1
         f = wire.send(tiles.at[1, high], tiles.at[2, high], at.down["x"])
         yield start + 2 * block, a2
+        ready(3)
         yield start + 2 * block, b2
+        ready(1)
         yield start + 3 * block, e
         yield start + 3 * block, f
+        ready(2)
     else:
         a = wire.send(own, tiles.at[3], at.up["x"])
         b = wire.send(own, tiles.at[1], at.down["x"])
@@ -210,25 +221,6 @@
     yield start + 4 * block, d2
 
 
-def comm_call(body, inputs, outs, scratch, copies, locals_, number, sent_bytes, name):
-    return pl.pallas_call(
-        body,
-        out_shape=outs,
-        in_specs=[pl.BlockSpec(memory_space=pl.ANY)] * len(inputs),
-        out_specs=[pl.BlockSpec(memory_space=pl.ANY)] * len(outs),
-        scratch_shapes=[
-            *scratch,
-            pltpu.SemaphoreType.DMA((copies,)),
-            pltpu.SemaphoreType.DMA((copies,)),
-            pltpu.SemaphoreType.DMA((max(1, locals_),)),
-        ],
-        compiler_params=pltpu.CompilerParams(
-            collective_id=number, has_side_effects=True, vmem_limit_bytes=8 << 20
-        ),
-        name=name,
-    )(*inputs)
-
-
 def like(shape, dtype=BF16):
     return jax.ShapeDtypeStruct(shape, dtype)
 
@@ -236,157 +228,282 @@
 GATHER_COPIES = 13
 
 
-def first_gather(tokens, pos, qkv, out):
-    def body(tok, pos_in, qkv_in, out_in, tiles, spots, qkv_all, out_all,
-             tok_v, pos_v, qkv_v, out_v, ss, rs, ls):
+def layer_norm(row_data, gain_vector):
+    row_data = row_data.astype(F32)
+    centered = row_data - jnp.mean(row_data, axis=-1, keepdims=True)
+    spread = jnp.mean(centered * centered, axis=-1, keepdims=True)
+    return centered * lax.rsqrt(spread + 1e-06) * gain_vector
+
+
+def gelu(v):
+    return v * (0.5 + 0.5 * lax.erf(v * 0.5**0.5))
+
+
+def dot(a, b):
+    return jnp.dot(a, b, preferred_element_type=F32)
+
+
+def dot_nt(a, b):
+    return lax.dot_general(a, b, (((1,), (1,)), ((), ())), preferred_element_type=F32)
+
+
+def ring(wire, own, arrive, to_next, to_far, up, down, t, dt, ready):
+    before, after, far = arrive
+    rows = own.shape[0] // 2
+    low, high = pl.ds(0, rows), pl.ds(rows, rows)
+    a = wire.send(own, to_next, up)
+    b = wire.send(own, to_next, down)
+    yield t + dt, a
+    e = wire.send(before.at[low], to_far[0].at[low], up)
+    ready(0)
+    yield t + dt, b
+    f = wire.send(after.at[high], to_far[1].at[high], down)
+    ready(1)
+    yield t + 2 * dt, e
+    yield t + 2 * dt, f
+    ready(2)
+
+
+def gather_fine(wire, at, whole, half, first, times, late, siblings):
+    c, zh, y, yf = at.core, at.zh, at.y, lax.rem(at.y + 2, 4)
+    t, dt = times
+
+    def cell(zr, zhi, yi):
+        return whole.at[zr, zhi, yi, c, half]
+
+    def share(ref):
+        siblings.append(wire.send(ref, ref, at.sibling))
+
+    def over_z(yi, t, ready):
+        return ring(
+            wire, cell(0, zh, yi), (cell(1, at.zhm, yi), cell(1, at.zhp, yi), cell(0, 1 - zh, yi)),
+            cell(1, zh, yi), (cell(0, at.zhm, yi), cell(0, at.zhp, yi)), at.up["z"], at.down["z"], t, dt, ready,
+        )
+
+    def over_y(zr, zhi, t, ready):
+        return ring(
+            wire, cell(zr, zhi, y), (cell(zr, zhi, at.ym), cell(zr, zhi, at.yp), cell(zr, zhi, yf)),
+            cell(zr, zhi, y), (cell(zr, zhi, at.ym), cell(zr, zhi, at.yp)), at.up["y"], at.down["y"], t, dt, ready,
+        )
+
+    order = [at.ym, at.yp, yf] if first == "y" else [(1, at.zhm), (1, at.zhp), (0, 1 - zh)]
+
+    def second(n, t):
+        if first == "y":
+            yi = y if n < 0 else order[n]
+            share(cell(0, zh, yi))
+            got = [cell(1, at.zhm, yi), cell(1, at.zhp, yi), cell(0, 1 - zh, yi)]
+            stream = over_z(yi, t, lambda m: share(got[m]))
+        else:
+            place = (0, zh) if n < 0 else order[n]
+            share(cell(*place, y))
+            got = [cell(*place, at.ym), cell(*place, at.yp), cell(*place, yf)]
+            stream = over_y(*place, t, lambda m: share(got[m]))
+        late.append((next(stream), stream))
+
+    ready = lambda n: second(n, t + dt * (1.5 + 1.5 * n))
+    stream = over_z(y, t, ready) if first == "z" else over_y(0, zh, t, ready)
+    step = next(stream)
+    second(-1, t)
+    while step is not None:
+        yield step
+        step = next(stream, None)
+
+
+def front_kernel(tokens, pos, qkv, out, ffn_in, down, gain_one, gain_two, number):
+    width = tokens.shape[1]
+    chunk, chunks = 512, width // 512
+    scale = 128.0**-0.5
+
+    def norm(rows, gain):
+        return layer_norm(rows, gain[...]).astype(BF16)
+
+    def body(tok, pos_in, qkv_in, out_in, in_in, down_in, gain1, gain2,
+             hidden, tiles_out, spots, in_all, down_all,
+             tiles, normed, qkv_all, out_all, in_v, down_v, pos_v, keys, theirs, queries,
+             tops, sums, parts, att, terms, got, across, mine, ss, rs, ls):
         at = Spot()
-        loads = [
-            pltpu.make_async_copy(tok, tok_v, ls.at[0]),
-            pltpu.make_async_copy(pos_in, pos_v, ls.at[1]),
-            pltpu.make_async_copy(qkv_in, qkv_v, ls.at[2]),
-            pltpu.make_async_copy(out_in, out_v, ls.at[3]),
+        zh, y, c = at.zh, at.y, at.core
+        copies = [
+            (tok, tiles.at[0]),
+            (qkv_in.at[0], qkv_all.at[0, zh, y, c, 0]),
+            (qkv_in.at[1], qkv_all.at[0, zh, y, c, 1]),
+            (pos_in, pos_v),
+            (out_in.at[0], out_all.at[0, zh, y, c, 0]),
+            (out_in.at[1], out_all.at[0, zh, y, c, 1]),
+            (in_in, in_v),
+            (down_in, down_v),
         ]
+        loads = [pltpu.make_async_copy(src, dst, ls.at[n]) for n, (src, dst) in enumerate(copies)]
         for load in loads:
             load.start()
         greet([at.up["x"], at.down["x"], at.up["y"], at.down["y"], at.up["z"], at.down["z"], at.sibling])
         for load in loads:
             load.wait()
-        stores = [
-            pltpu.make_async_copy(tok_v, tiles.at[0], ls.at[4]),
-            pltpu.make_async_copy(pos_v, spots.at[0], ls.at[5]),
-            *[
-                pltpu.make_async_copy(src.at[h], dst.at[0, at.zh, at.y, at.core, h], ls.at[6 + 2 * n + h])
-                for n, (src, dst) in enumerate(((qkv_v, qkv_all), (out_v, out_all)))
-                for h in range(2)
-            ],
+        copies = [
+            (pos_v, spots.at[0]),
+            (in_v.at[0], in_all.at[0, zh, y, c, 0]),
+            (in_v.at[1], in_all.at[0, zh, y, c, 1]),
+            (down_v.at[0], down_all.at[0, zh, y, c, 0]),
+            (down_v.at[1], down_all.at[0, zh, y, c, 1]),
         ]
+        stores = [pltpu.make_async_copy(src, dst, ls.at[n]) for n, (src, dst) in enumerate(copies)]
         for store in stores:
             store.start()
         wire = Wire(ss, rs)
+        late, siblings = [], []
+
+        def norm_tile(s):
+            normed[pl.ds(s * 128, 128), :] = norm(tiles[s], gain1)
+
+        def main():
+            yield 1, None
+            norm_tile(0)
+            yield 21, None
+            assert len(siblings) == 32
+            for copy in siblings:
+                yield 21, copy
+            columns = [pl.ds(h * 384 + 128, 256) for h in range(2)]
+            swaps = []
+            for r in range(2):
+                for h in range(2):
+                    weight = qkv_all[r, :, :, :, :, :, columns[h]].reshape(width, 256)
+                    keys[r, h] = dot(normed[...], weight).astype(BF16)
+                    swaps.append(wire.send(keys.at[r, h], theirs.at[1 - r, h], at.pair))
+            yield 26, None
+
+            def queries_of(n, carry):
+                column = pl.ds(pl.multiple_of(lax.rem(n, 2) * 384, 128), 128)
+                weight = qkv_all[lax.div(n, 2), :, :, :, :, :, column].reshape(width, 128)
+                queries[n] = dot(normed[...], weight).astype(BF16)
+                return carry
+
+            lax.fori_loop(0, 4, queries_of, 0)
+            yield 27, None
+
+            def scored(n, rows, pair):
+                scores = dot_nt(queries[n, rows, :], pair[:, pl.ds(0, 128)]) * scale
+                top = jnp.max(scores, axis=-1, keepdims=True)
+                weights = jnp.exp(scores - top)
+                part = dot(weights.astype(BF16), pair[:, pl.ds(128, 128)])
+                return top, jnp.sum(weights, axis=-1, keepdims=True), part
+
+            for n in range(4):
+                def own_keys(m, carry, n=n):
+                    rows = pl.ds(pl.multiple_of(m * 128, 128), 128)
+                    top, total, part = scored(n, rows, keys.at[n // 2, n % 2])
+                    tops[n, rows, :] = top
+                    sums[n, rows, :] = total
+                    parts[n, rows, :] = part
+                    return carry
+
+                lax.fori_loop(0, 4, own_keys, 0)
+                yield 28 + n, None
+
+            for k, n in enumerate((2, 3, 0, 1)):
+                yield 27 + 5.6 * (k + 1), swaps[k]
+
+                def their_keys(m, carry, n=n):
+                    rows = pl.ds(pl.multiple_of(m * 128, 128), 128)
+                    top, total, part = scored(n, rows, theirs.at[n // 2, n % 2])
+                    best = jnp.maximum(top, tops[n, rows, :])
+                    ours, new = jnp.exp(tops[n, rows, :] - best), jnp.exp(top - best)
+                    total = total * new + sums[n, rows, :] * ours
+                    value = (part * new + parts[n, rows, :] * ours) / total
+                    att[rows, pl.ds(n * 128, 128)] = value.astype(BF16)
+                    return carry
+
+                lax.fori_loop(0, 4, their_keys, 0)
+            for j in range(chunks):
+                late.append(((50 + 0.6 * j, None), mix(j)))
+
+        left = [chunks]
+
+        def mix(j):
+            zhi, yi = j // 2, (j % 2) * 2
+            first = out_all[0, zhi, pl.ds(yi, 2)].reshape(chunk, 256)
+            second = out_all[1, zhi, pl.ds(yi, 2)].reshape(chunk, 256)
+            mixed = dot_nt(att[:, pl.ds(0, 256)], first) + dot_nt(att[:, pl.ds(256, 256)], second)
+            terms[j] = mixed.astype(BF16).reshape(4, 128, chunk)
+            yield from scatter_x(wire, at, terms.at[j], got.at[j], across.at[j], 52 + 5.6 * j, 1.4)
+            columns = pl.ds(j * chunk, chunk)
+            total = tiles[0, :, columns].astype(F32) + terms[j, 0].astype(F32)
+            for n in range(3):
+                total = total + got[j, n].astype(F32)
+            hidden[:, columns] = total.astype(BF16)
+            left[0] -= 1
+            if left[0] == 0:
+                mine[...] = norm(hidden[...], gain2)
+                last = pltpu.make_async_copy(mine, tiles_out.at[0], ls.at[5])
+                last.start()
+                stores.append(last)
+                stream = gather_x(wire, at, mine, tiles_out, 2, 77, 5.7)
+                late.append((next(stream), stream))
+
+        def after(t, stream):
+            yield t, None
+            yield from stream
+
         run_streams([
             gather_x(wire, at, pos_v, spots, 1, 0, 2),
-            gather_x(wire, at, tok_v, tiles, 2, 0, 5.7),
-            gather_weight(wire, at, qkv_v.at[0], stores[2], qkv_all, 0, "y", 0, 1.1),
-            gather_weight(wire, at, qkv_v.at[1], stores[3], qkv_all, 1, "z", 0, 1.1),
-            gather_weight(wire, at, out_v.at[0], stores[4], out_all, 0, "y", 1, 1.4),
-            gather_weight(wire, at, out_v.at[1], stores[5], out_all, 1, "z", 1, 1.4),
-        ])
-        for store in stores[:2]:
+            gather_x(wire, at, tiles.at[0], tiles, 2, 0, 5.7, norm_tile),
+            gather_fine(wire, at, qkv_all, 0, "y", (0, 3.2), late, siblings),
+            gather_fine(wire, at, qkv_all, 1, "z", (0, 3.2), late, siblings),
+            main(),
+            after(10, gather_weight(wire, at, out_all.at[0, zh, y, c, 0], None, out_all, 0, "y", 10, 0.8)),
+            after(10, gather_weight(wire, at, out_all.at[0, zh, y, c, 1], None, out_all, 1, "z", 10, 0.8)),
+            after(13, gather_weight(wire, at, in_v.at[0], stores[1], in_all, 0, "y", 16, 2.8, 27)),
+            after(13.5, gather_weight(wire, at, in_v.at[1], stores[2], in_all, 1, "y", 18, 2.8, 38)),
+            after(26.5, gather_weight(wire, at, down_v.at[0], stores[3], down_all, 0, "z", 43, 2.8, 52)),
+            after(26.6, gather_weight(wire, at, down_v.at[1], stores[4], down_all, 1, "z", 46, 2.8, 58)),
+        ], late)
+        for store in [stores[0], *stores[5:]]:
             store.wait()
         for copy in wire.sent:
             copy.wait_send()
 
-    outs = [
-        like((4, *tokens.shape)),
-        like((4, *pos.shape), jnp.int32),
-        like((2, 2, 4, 2, *qkv.shape)),
-        like((2, 2, 4, 2, *out.shape)),
-    ]
-    scratch = [
-        pltpu.VMEM(tokens.shape, BF16),
-        pltpu.VMEM(pos.shape, jnp.int32),
-        pltpu.VMEM(qkv.shape, BF16),
-        pltpu.VMEM(out.shape, BF16),
-    ]
-    return comm_call(body, [tokens, pos, qkv, out], outs, scratch,
-                     9 + 4 * GATHER_COPIES, 10, 1, 0, "gather_first")
-
-
-def pair_swap(mine, number, name):
-    def body(src, dst, ss, rs, ls):
-        at = Spot()
-        greet([at.pair])
-        wire = Wire(ss, rs)
-        copy = wire.send(src.at[1], dst, at.pair)
-        copy.wait()
-
-    return comm_call(body, [mine], [like(mine.shape[1:])], [], 1, 0, number, 0, name)[0]
-
-
-def scatter_and_weight(terms, weight, number, name):
-    def body(src, w_in, got, passing, w_all, w_v, ss, rs, ls):
-        at = Spot()
-        load = pltpu.make_async_copy(w_in, w_v, ls.at[0])
-        load.start()
-        greet([at.up["x"], at.down["x"], at.up["y"], at.down["y"], at.up["z"], at.down["z"], at.sibling])
-        load.wait()
-        stores = [
-            pltpu.make_async_copy(w_v.at[h], w_all.at[0, at.zh, at.y, at.core, h], ls.at[1 + h])
-            for h in range(2)
-        ]
-        for store in stores:
-            store.start()
-        wire = Wire(ss, rs)
-        run_streams([
-            scatter_x(wire, at, src, got, passing, 0, 5.7),
-            gather_weight(wire, at, w_v.at[0], stores[0], w_all, 0, "y", 0, 1.4),
-            gather_weight(wire, at, w_v.at[1], stores[1], w_all, 1, "z", 0, 1.4),
-        ])
-        for copy in wire.sent:
-            copy.wait_send()
-
-    rows, width = terms.shape[1:]
-    outs = [
-        like((3, rows, width)),
-        like((2, rows // 2, width)),
-        like((2, 2, 4, 2, *weight.shape)),
-    ]
-    got, _, whole = comm_call(body, [terms, weight], outs, [pltpu.VMEM(weight.shape, BF16)],
-                              6 + 2 * GATHER_COPIES, 3, number, 0, name)
-    return got, whole
-
-
-def gather_and_weight(block, weight, number, name):
-    def body(src, w_in, tiles, w_all, src_v, w_v, ss, rs, ls):
-        at = Spot()
-        loads = [
-            pltpu.make_async_copy(src, src_v, ls.at[0]),
-            pltpu.make_async_copy(w_in, w_v, ls.at[1]),
-        ]
-        for load in loads:
-            load.start()
-        greet([at.up["x"], at.down["x"], at.up["y"], at.down["y"], at.up["z"], at.down["z"], at.sibling])
-        for load in loads:
-            load.wait()
-        stores = [pltpu.make_async_copy(src_v, tiles.at[0], ls.at[2])] + [
-            pltpu.make_async_copy(w_v.at[h], w_all.at[0, at.zh, at.y, at.core, h], ls.at[3 + h])
-            for h in range(2)
-        ]
-        for store in stores:
-            store.start()
-        wire = Wire(ss, rs)
-        run_streams([
-            gather_x(wire, at, src_v, tiles, 2, 0, 5.7),
-            gather_weight(wire, at, w_v.at[0], stores[1], w_all, 0, "y", 0, 1.4),
-            gather_weight(wire, at, w_v.at[1], stores[2], w_all, 1, "z", 0, 1.4),
-        ])
-        stores[0].wait()
-        for copy in wire.sent:
-            copy.wait_send()
-
-    outs = [like((4, *block.shape)), like((2, 2, 4, 2, *weight.shape))]
-    scratch = [pltpu.VMEM(block.shape, BF16), pltpu.VMEM(weight.shape, BF16)]
-    return comm_call(body, [block, weight], outs, scratch,
-                     6 + 2 * GATHER_COPIES, 5, number, 0, name)
-
-
-def layer_norm(row_data, gain_vector):
-    row_data = row_data.astype(F32)
-    centered = row_data - jnp.mean(row_data, axis=-1, keepdims=True)
-    spread = jnp.mean(centered * centered, axis=-1, keepdims=True)
-    return centered * lax.rsqrt(spread + 1e-06) * gain_vector
-
-
-def gelu(v):
-    return v * (0.5 + 0.5 * lax.erf(v * 0.5**0.5))
-
-
-def dot(a, b):
-    return jnp.dot(a, b, preferred_element_type=F32)
-
-
-def dot_nt(a, b):
-    return lax.dot_general(a, b, (((1,), (1,)), ((), ())), preferred_element_type=F32)
+    hbm, vmem = pl.BlockSpec(memory_space=pl.ANY), pl.BlockSpec(memory_space=pltpu.VMEM)
+    inputs = [tokens, pos, qkv, out, ffn_in, down, gain_one, gain_two]
+    copies = 4 + 3 + 6 + 2 * 36 + 6 * GATHER_COPIES + 6 * chunks + 6
+    return pl.pallas_call(
+        body,
+        out_shape=[
+            like(tokens.shape),
+            like((4, *tokens.shape)),
+            like((4, *pos.shape), jnp.int32),
+            like((2, 2, 4, 2, *ffn_in.shape)),
+            like((2, 2, 4, 2, *down.shape)),
+        ],
+        in_specs=[hbm] * 6 + [vmem] * 2,
+        out_specs=[vmem] + [hbm] * 4,
+        scratch_shapes=[
+            pltpu.VMEM((4, *tokens.shape), BF16),
+            pltpu.VMEM((512, width), BF16),
+            pltpu.VMEM((2, 2, 4, 2, *qkv.shape), BF16),
+            pltpu.VMEM((2, 2, 4, 2, *out.shape), BF16),
+            pltpu.VMEM(ffn_in.shape, BF16),
+            pltpu.VMEM(down.shape, BF16),
+            pltpu.VMEM(pos.shape, jnp.int32),
+            pltpu.VMEM((2, 2, 512, 256), BF16),
+            pltpu.VMEM((2, 2, 512, 256), BF16),
+            pltpu.VMEM((4, 512, 128), BF16),
+            pltpu.VMEM((4, 512, 1), F32),
+            pltpu.VMEM((4, 512, 1), F32),
+            pltpu.VMEM((4, 512, 128), F32),
+            pltpu.VMEM((512, 512), BF16),
+            pltpu.VMEM((chunks, 4, 128, chunk), BF16),
+            pltpu.VMEM((chunks, 3, 128, chunk), BF16),
+            pltpu.VMEM((chunks, 2, 64, chunk), BF16),
+            pltpu.VMEM(tokens.shape, BF16),
+            pltpu.SemaphoreType.DMA((copies,)),
+            pltpu.SemaphoreType.DMA((copies,)),
+            pltpu.SemaphoreType.DMA((8,)),
+        ],
+        compiler_params=pltpu.CompilerParams(
+            collective_id=number, has_side_effects=True, vmem_limit_bytes=66_000_000
+        ),
+        name="attention_front",
+    )(*inputs)
 
 
 def tail_kernel(table, normed, hidden, placed, in_all, down_all, expert_in, expert_out, number):
@@ -620,34 +737,12 @@
     earlier = jnp.sum(dot(before, one_hot) * one_hot.astype(F32), axis=1)
     pos = (chosen * slots + earlier.astype(jnp.int32))[None, :]
 
-    heads, head_dim = qkv_weight.shape[1], qkv_weight.shape[3]
-    qkv_width = heads * 3 * head_dim
-    tiles, spots, qkv_all, out_all = first_gather(
-        tokens, pos, qkv_weight.reshape(2, -1, qkv_width), out_weight.T.reshape(2, -1, out_weight.shape[0])
+    qkv_width = qkv_weight.shape[1] * 3 * qkv_weight.shape[3]
+    hidden, tiles, spots, in_all, down_all = front_kernel(
+        tokens, pos, qkv_weight.reshape(2, -1, qkv_width), out_weight.T.reshape(2, -1, out_weight.shape[0]),
+        ffn_in.reshape(2, -1, ffn_in.shape[1]), ffn_out.T.reshape(2, -1, ffn_out.shape[0]),
+        ln1_gain[None, :], ln2_gain[None, :], 1,
     )
-    normed = layer_norm(tiles.reshape(4 * count, width), ln1_gain).astype(BF16)
-    qkv_all = qkv_all.reshape(2, width, qkv_width)
-    projected = jnp.stack([dot(normed, qkv_all[n]).astype(BF16) for n in range(2)])
-    other = pair_swap(projected, 2, "swap_heads")
-    image = jnp.concatenate([projected[0], other]).reshape(-1, heads, 3, head_dim)
-    scores = jnp.einsum(
-        "qhd,khd->hqk", image[:, :, 0], image[:, :, 1], preferred_element_type=F32
-    ) * head_dim ** (-0.5)
-    weights = jnp.exp(scores - jnp.max(scores, axis=-1, keepdims=True))
-    probabilities = (weights / jnp.sum(weights, axis=-1, keepdims=True)).astype(BF16)
-    attended = jnp.einsum("hqk,khd->qhd", probabilities, image[:, :, 2], preferred_element_type=F32)
-    attended = attended.astype(BF16).reshape(2, 4 * count, heads * head_dim)
-    other = pair_swap(attended, 3, "swap_attended")
-    out_all = out_all.reshape(2, width, -1)
-    mixed = dot_nt(attended[0], out_all[0]) + dot_nt(other, out_all[1])
-    mixed = mixed.astype(BF16).reshape(4, count, width)
-    got, in_all = scatter_and_weight(mixed, ffn_in.reshape(2, -1, ffn_in.shape[1]), 4, "scatter_heads")
-    hidden = (
-        tokens.astype(F32) + mixed[0].astype(F32) + got[0].astype(F32) + got[1].astype(F32) + got[2].astype(F32)
-    ).astype(BF16)
-    normed_mine = layer_norm(hidden, ln2_gain).astype(BF16)
-    down = ffn_out.T
-    tiles, down_all = gather_and_weight(normed_mine, down.reshape(2, -1, down.shape[1]), 5, "gather_normed")
     normed = tiles.reshape(4 * count, width)
 
     zh, y, core, x = (lax.axis_index(name) for name in ("zh", "y", "core", "x"))

time: 277 us -> 255 us (0.921)
  local copies, waits for them, and re-layouts: 27.3 us -> 8.2 us
  matrix products: 19.2 us -> 2.6 us
  Pallas kernels: 224 us -> 240 us
    pallas_call x5 -> x1, Pallas kernels: 131 us -> 147 us  [front_kernel(): pl.pallas_call(body, out_shape=[like(tokens.shape), like((4, *tokens.shap...]
    unnamed x27 -> x5, local copies, waits for them, and re-layouts: 15.1 us -> 2.98 us
    sub x1 -> x0, matrix products: 7.2 us -> none  [shards(): weights = jnp.exp(scores - jnp.max(scores, axis=-1, keepdims=True))]
    dot_general x3 -> x0, matrix products: 5.81 us -> none  [the longest x1 4.3 us: shards(): jnp.einsum('hqk,khd->qhd', probabilities, image[:, :, 2], preferred_eleme...]
    slice x3 -> x0, local copies, waits for them, and re-layouts: 4.61 us -> none  [the longest x1 3.4 us: shards(): qkv_all[n]]
    dot_general x4 -> x2, matrix products: 6.19 us -> 2.6 us  [dot(): return jnp.dot(a, b, preferred_element_type=F32)]
where the time goes in v1:
time: 255 us
  Pallas kernels  240 us (94%)
  local copies, waits for them, and re-layouts  8.2 us (3%)
  other arithmetic  4.01 us (2%)
  matrix products  2.6 us (1%)
    pallas_call x1, Pallas kernels, front_kernel(): pl.pallas_call(body, out_shape=[like(tokens.shape), like((4, *tokens.shap...  147 us
    pallas_call x1, Pallas kernels, tail_kernel(): pl.pallas_call(body, out_shape=like((128, width)), in_specs=[pl.BlockSpec...  93 us

profile of v1, /device:TPU:1, one launch (start us, length us, event | category | flops | bytes accessed | tf_op | source)
XLA Modules:
  0.0 254.6 jit_solution(9721703231645543853)
XLA Ops:
  0.0 0.9 fusion
  0.9 1.3 bitcast_add_fusion.pos_in
  2.2 0.1 add_multiply_fusion.1
  2.3 0.1 add_multiply_fusion
  2.4 0.1 iota_add_fusion.1
  2.5 0.1 iota_add_fusion
  2.6 1.6 copy.16
  4.1 1.0 copy.15
  5.1 0.9 reshape.119.qkv_in
  6.0 1.8 copy.17
  7.8 146.6 %attention_front.1 = (bf16[128,2048]{1,0:T(8,128)(2,1)}, bf16[4,128,2048]{2,1,0:T(8,128)(2,1)}, s32[4,1,128]{2,1,0:T(1,128)}, bf16[2,2,4,2,2,64,1024]{6,5,4,3,2,...) custom-call(bf16[128,2048]{1,0:T(8,128)(2,1)} %tok.1, s32[1,128]{1,0:T(1,128)} %bitcast_add_fusion.pos_in, ...), custom_call_target="tpu_custom_call" | custom-call | tf_op jit(solution)/shard_map/attention_front/pallas_call | solution.py:468
  154.4 0.0 copy-start
  154.4 1.0 broadcast_compare_fusion.1
  155.4 0.9 broadcast_compare_fusion
  156.3 0.2 broadcast_and_fusion
  156.5 0.4 and_convert_fusion
  156.8 0.1 copy.26
  156.9 1.0 copy.18
  157.9 0.0 copy-done
  157.9 1.7 convolution_convert_fusion
  159.6 93.0 %experts_and_dense.1 = bf16[128,2048]{1,0:T(8,128)(2,1)} custom-call(bf16[2,4,2,16,2048]{4,3,2,1,0:T(8,128)(2,1)} %bitcast.37, bf16[512,2048]{1,0:T(8,128)(2,1)} %bitcast.31, bf16[128,2048]{1,0:T(8,128)(2,1)} %get-tuple-element.12.hid, bf16[512,512]{1,0:T(8,128)(2,1)} %bitcast.38, bf16[2,2048,1024]{2,1,0:T(8,128)(2,1)} %bitcast.35, ...), custom_call_target="tpu_custom_call" | custom-call | tf_op jit(solution)/shard_map/experts_and_dense/pallas_call | solution.py:695
  252.7 1.9 copy.28
  (7 shorter events, 0.1 us)
Async XLA Ops:
  154.4 3.5 %copy-start = (bf16[4,128,2048]{2,1,0:T(8,128)(2,1)S(1)}, bf16[4,128,2048]{2,1,0:T(8,128)(2,1)}, u32[]{:S(2)}) copy-start(bf16[4,128,2048]{2,1,0:T(8,128)(2,1)} %get-tuple-element.11) | copy-start | bytes 6291460

commit v2 on v1

--- a/solution.py
+++ b/solution.py
@@ -90,90 +90,87 @@
             count += 1
 
 
-def gather_weight(wire, at, own, local, whole, half, first, start, block, hold=None):
+def gather_weight(wire, at, own, local, whole, half, first, times):
     c, zh, y = at.core, at.zh, at.y
+    near, relayed, hold, grouped, last = times
     rows = own.shape[0] // 2
     low, high = pl.ds(0, rows), pl.ds(rows, rows)
     if first == "y":
         a = wire.send(own, whole.at[0, zh, y, c, half], at.up["y"])
         b = wire.send(own, whole.at[0, zh, y, c, half], at.down["y"])
-        yield start + 2 * block, a
+        yield near, a
         slot = whole.at[0, zh, at.ym, c, half, low]
         e = wire.send(slot, slot, at.up["y"])
-        yield start + 2 * block, b
+        yield near, b
         slot = whole.at[0, zh, at.yp, c, half, high]
         f = wire.send(slot, slot, at.down["y"])
-        yield start + 3 * block, e
-        yield start + 3 * block, f
+        yield relayed, e
+        yield relayed, f
         if local is not None:
             local.wait()
-        if hold is not None:
-            yield hold, None
-            start = hold
+        yield hold, None
         group = whole.at[0, zh, :, c, half]
         far = whole.at[1, zh, :, c, half]
         g = wire.send(group, far, at.up["z"])
         h = wire.send(group, far, at.down["z"])
         s = [wire.send(group, group, at.sibling)]
-        yield start + 11 * block, g
+        yield grouped, g
         lower = pl.ds(0, 2)
         i = wire.send(
             whole.at[1, at.zhm, lower, c, half], whole.at[0, at.zhm, lower, c, half], at.up["z"]
         )
         s.append(wire.send(whole.at[1, at.zhm, :, c, half], whole.at[1, at.zhm, :, c, half], at.sibling))
-        yield start + 11 * block, h
+        yield grouped, h
         upper = pl.ds(2, 2)
         j = wire.send(
             whole.at[1, at.zhp, upper, c, half], whole.at[0, at.zhp, upper, c, half], at.down["z"]
         )
         s.append(wire.send(whole.at[1, at.zhp, :, c, half], whole.at[1, at.zhp, :, c, half], at.sibling))
-        yield start + 15 * block, i
+        yield last, i
         slot = whole.at[0, 1 - zh, lower, c, half]
         s.append(wire.send(slot, slot, at.sibling))
-        yield start + 15 * block, j
+        yield last, j
         slot = whole.at[0, 1 - zh, upper, c, half]
         s.append(wire.send(slot, slot, at.sibling))
     else:
         a = wire.send(own, whole.at[1, zh, y, c, half], at.up["z"])
         b = wire.send(own, whole.at[1, zh, y, c, half], at.down["z"])
-        yield start + 2 * block, a
+        yield near, a
         e = wire.send(
             whole.at[1, at.zhm, y, c, half, low], whole.at[0, at.zhm, y, c, half, low], at.up["z"]
         )
-        yield start + 2 * block, b
+        yield near, b
         f = wire.send(
             whole.at[1, at.zhp, y, c, half, high], whole.at[0, at.zhp, y, c, half, high], at.down["z"]
         )
-        yield start + 3 * block, e
-        yield start + 3 * block, f
+        yield relayed, e
+        yield relayed, f
         if local is not None:
             local.wait()
-        if hold is not None:
-            yield hold, None
-            start = hold
+        yield hold, None
         group = whole.at[:, :, y, c, half]
         g = wire.send(group, group, at.up["y"])
         h = wire.send(group, group, at.down["y"])
         s = [wire.send(group, group, at.sibling)]
-        yield start + 11 * block, g
+        yield grouped, g
         slot = whole.at[0, :, at.ym, c, half]
         i = wire.send(slot, slot, at.up["y"])
         slot = whole.at[:, :, at.ym, c, half]
         s.append(wire.send(slot, slot, at.sibling))
-        yield start + 11 * block, h
+        yield grouped, h
         slot = whole.at[1, :, at.yp, c, half]
         j = wire.send(slot, slot, at.down["y"])
         slot = whole.at[:, :, at.yp, c, half]
         s.append(wire.send(slot, slot, at.sibling))
         across = lax.rem(y + 2, 4)
-        yield start + 15 * block, i
+        yield last, i
         slot = whole.at[0, :, across, c, half]
         s.append(wire.send(slot, slot, at.sibling))
-        yield start + 15 * block, j
+        yield last, j
         slot = whole.at[1, :, across, c, half]
         s.append(wire.send(slot, slot, at.sibling))
     for n, copy in enumerate(s):
-        yield start + 15 * block + 2 + n / 8, copy
+        yield last + 2 + n / 8, copy
 
 
 def gather_x(wire, at, own, tiles, parts, start, block, ready=lambda s: None):
@@ -204,21 +201,22 @@
         yield start + 2 * block, e
 
 
-def scatter_x(wire, at, terms, got, passing, start, block):
+def scatter_x(wire, at, terms, got, passing, times):
+    first, near, last = times
     half = terms.shape[1] // 2
     low, high = pl.ds(0, half), pl.ds(half, half)
     c1 = wire.send(terms.at[2, low], passing.at[0], at.up["x"])
     c2 = wire.send(terms.at[2, high], passing.at[1], at.down["x"])
     a = wire.send(terms.at[1], got.at[0], at.up["x"])
     b = wire.send(terms.at[3], got.at[1], at.down["x"])
-    yield start + block, c1
+    yield first, c1
     d1 = wire.send(passing.at[0], got.at[2, low], at.up["x"])
-    yield start + block, c2
+    yield first, c2
     d2 = wire.send(passing.at[1], got.at[2, high], at.down["x"])
-    yield start + 3 * block, a
-    yield start + 3 * block, b
-    yield start + 4 * block, d1
-    yield start + 4 * block, d2
+    yield near, a
+    yield near, b
+    yield last, d1
+    yield last, d2
 
 
 def like(shape, dtype=BF16):
@@ -338,8 +336,8 @@
         for load in loads:
             load.start()
         greet([at.up["x"], at.down["x"], at.up["y"], at.down["y"], at.up["z"], at.down["z"], at.sibling])
-        for load in loads:
-            load.wait()
+        for n in (0, 1, 2, 3, 6, 7):
+            loads[n].wait()
         copies = [
             (pos_v, spots.at[0]),
             (in_v.at[0], in_all.at[0, zh, y, c, 0]),
@@ -347,7 +345,7 @@
             (down_v.at[0], down_all.at[0, zh, y, c, 0]),
             (down_v.at[1], down_all.at[0, zh, y, c, 1]),
         ]
-        stores = [pltpu.make_async_copy(src, dst, ls.at[n]) for n, (src, dst) in enumerate(copies)]
+        stores = [pltpu.make_async_copy(src, dst, ls.at[8 + n]) for n, (src, dst) in enumerate(copies)]
         for store in stores:
             store.start()
         wire = Wire(ss, rs)
@@ -359,6 +357,9 @@
         def main():
             yield 1, None
             norm_tile(0)
+            yield 11.2, None
+            loads[4].wait()
+            loads[5].wait()
             yield 21, None
             assert len(siblings) == 32
             for copy in siblings:
@@ -425,7 +426,7 @@
             second = out_all[1, zhi, pl.ds(yi, 2)].reshape(chunk, 256)
             mixed = dot_nt(att[:, pl.ds(0, 256)], first) + dot_nt(att[:, pl.ds(256, 256)], second)
             terms[j] = mixed.astype(BF16).reshape(4, 128, chunk)
-            yield from scatter_x(wire, at, terms.at[j], got.at[j], across.at[j], 52 + 5.6 * j, 1.4)
+            yield from scatter_x(wire, at, terms.at[j], got.at[j], across.at[j], (53.4 + 4.2 * j, 56.2 + 4.2 * j, 69.5 + 1.4 * j))
             columns = pl.ds(j * chunk, chunk)
             total = tiles[0, :, columns].astype(F32) + terms[j, 0].astype(F32)
             for n in range(3):
@@ -434,7 +435,7 @@
             left[0] -= 1
             if left[0] == 0:
                 mine[...] = norm(hidden[...], gain2)
-                last = pltpu.make_async_copy(mine, tiles_out.at[0], ls.at[5])
+                last = pltpu.make_async_copy(mine, tiles_out.at[0], ls.at[13])
                 last.start()
                 stores.append(last)
                 stream = gather_x(wire, at, mine, tiles_out, 2, 77, 5.7)
@@ -445,17 +446,17 @@
             yield from stream
 
         run_streams([
-            gather_x(wire, at, pos_v, spots, 1, 0, 2),
+            gather_x(wire, at, pos_v, spots, 1, 30, 20),
             gather_x(wire, at, tiles.at[0], tiles, 2, 0, 5.7, norm_tile),
             gather_fine(wire, at, qkv_all, 0, "y", (0, 3.2), late, siblings),
             gather_fine(wire, at, qkv_all, 1, "z", (0, 3.2), late, siblings),
             main(),
-            after(10, gather_weight(wire, at, out_all.at[0, zh, y, c, 0], None, out_all, 0, "y", 10, 0.8)),
-            after(10, gather_weight(wire, at, out_all.at[0, zh, y, c, 1], None, out_all, 1, "z", 10, 0.8)),
-            after(13, gather_weight(wire, at, in_v.at[0], stores[1], in_all, 0, "y", 16, 2.8, 27)),
-            after(13.5, gather_weight(wire, at, in_v.at[1], stores[2], in_all, 1, "y", 18, 2.8, 38)),
-            after(26.5, gather_weight(wire, at, down_v.at[0], stores[3], down_all, 0, "z", 43, 2.8, 52)),
-            after(26.6, gather_weight(wire, at, down_v.at[1], stores[4], down_all, 1, "z", 46, 2.8, 58)),
+            after(11.3, gather_weight(wire, at, out_all.at[0, zh, y, c, 0], None, out_all, 0, "z", (16.5, 20.9, 21.1, 38, 45))),
+            after(11.3, gather_weight(wire, at, out_all.at[0, zh, y, c, 1], None, out_all, 1, "z", (16.6, 20.9, 21.1, 38, 45))),
+            after(20.95, gather_weight(wire, at, in_v.at[0], stores[1], in_all, 0, "y", (29.5, 31.5, 55.3, 76, 85))),
+            after(20.95, gather_weight(wire, at, in_v.at[1], stores[2], in_all, 1, "y", (29.6, 31.6, 55.4, 80, 90))),
+            after(26.5, gather_weight(wire, at, down_v.at[0], stores[3], down_all, 0, "z", (55.2, 60, 60, 76.5, 85.5))),
+            after(26.6, gather_weight(wire, at, down_v.at[1], stores[4], down_all, 1, "z", (55.2, 60, 60, 80.5, 90.5))),
         ], late)
         for store in [stores[0], *stores[5:]]:
             store.wait()
@@ -497,7 +498,7 @@
             pltpu.VMEM(tokens.shape, BF16),
             pltpu.SemaphoreType.DMA((copies,)),
             pltpu.SemaphoreType.DMA((copies,)),
-            pltpu.SemaphoreType.DMA((8,)),
+            pltpu.SemaphoreType.DMA((14,)),
         ],
         compiler_params=pltpu.CompilerParams(
             collective_id=number, has_side_effects=True, vmem_limit_bytes=66_000_000
@@ -512,7 +513,7 @@
 
     def body(tab, nor, hid, pla, win, wdown, ein, eout, out,
              nor_v, hid_v, pla_v, win_v, wdown_v, ein_v, eout_v,
-             units, dense, xx, aside, passing, away, mine, hop, near, ahead, sib,
+             units, dense, xx, aside, passing, away, mine, hop, other, summed, both_sums, near, ahead, sib,
              terms, got, across, ss, rs, ls):
         at = Spot()
         cross = {"zh": 1 - at.zh, "zl": 1 - at.zl}
@@ -646,41 +647,41 @@
                 inside = pl.ds(n * tile, tile)
                 part = dot(units[...], eout_v[:, pl.ds(j * chunk + n * tile, tile)]).astype(BF16)
                 part = part.reshape(4, 4, 2, 16, tile)
-                mine[j, 0, :, :, :, inside] = part[0]
+                mine[j, :, :, :, inside] = part[0]
                 away[j, :, :, :, :, inside] = part[1:]
-            z1 = wire.send(away.at[j, 0], mine.at[j, 1], at.pair)
             z3 = wire.send(away.at[j, 2], hop.at[j], at.pair)
-            z2 = wire.send(away.at[j, 1], mine.at[j, 2], cross)
+            z1 = wire.send(away.at[j, 0], other.at[j], at.pair)
             t = 5.6 * j
-            yield t + 7, z3
-            f = wire.send(hop.at[j], mine.at[j, 3], cross)
-            yield t + 7, z1
-            yield t + 7, z2
-            yield t + 10, f
-            c = wire.send(mine.at[j, :, 2, 0], near.at[j, 0], at.down["y"])
-            d = wire.send(mine.at[j, :, 2, 1], near.at[j, 1], at.up["y"])
-            a = wire.send(mine.at[j, :, 1], ahead.at[j, :, 1], at.down["y"])
-            b = wire.send(mine.at[j, :, 3], ahead.at[j, :, 3], at.up["y"])
-            k0 = wire.send(mine.at[j, :, 0, 1], sib.at[j, :, 0], at.sibling)
-            yield t + 13, c
+            yield t + 5, z3
+            summed[j] = (away[j, 1].astype(F32) + hop[j].astype(F32)).astype(BF16)
+            f = wire.send(summed.at[j], both_sums.at[j, 1], cross)
+            yield t + 8, z1
+            both_sums[j, 0] = (mine[j].astype(F32) + other[j].astype(F32)).astype(BF16)
+            yield t + 9.5, f
+            c = wire.send(both_sums.at[j, :, 2, 0], near.at[j, 0], at.down["y"])
+            d = wire.send(both_sums.at[j, :, 2, 1], near.at[j, 1], at.up["y"])
+            a = wire.send(both_sums.at[j, :, 1], ahead.at[j, :, 1], at.down["y"])
+            b = wire.send(both_sums.at[j, :, 3], ahead.at[j, :, 3], at.up["y"])
+            k0 = wire.send(both_sums.at[j, :, 0, 1], sib.at[j, :, 0], at.sibling)
+            yield t + 12, c
             c2 = wire.send(near.at[j, 0], ahead.at[j, :, 2, 0], at.down["y"])
-            yield t + 13, d
+            yield t + 12, d
             d2 = wire.send(near.at[j, 1], ahead.at[j, :, 2, 1], at.up["y"])
-            yield t + 16, a
-            yield t + 16, b
-            yield t + 17, c2
-            yield t + 17, d2
+            yield t + 13.6, a
+            yield t + 13.6, b
+            yield t + 14.8, c2
+            yield t + 14.8, d2
             k1 = wire.send(ahead.at[j, :, pl.ds(1, 3), 1], sib.at[j, :, pl.ds(1, 3)], at.sibling)
-            yield t + 18.5, k0
-            yield t + 18.5, k1
+            yield t + 16.5, k0
+            yield t + 16.5, k1
             columns = pl.ds(j * chunk, chunk)
             first = jnp.concatenate(
-                [mine[j, :, pl.ds(0, 1), 0], ahead[j, :, pl.ds(1, 3), 0]], axis=1
-            ).reshape(256, chunk)
-            total = dense[:, columns] + dot(pla_v[:, pl.ds(0, 256)], first)
-            total = total + dot(pla_v[:, pl.ds(256, 256)], sib[j].reshape(256, chunk))
+                [both_sums[j, :, pl.ds(0, 1), 0], ahead[j, :, pl.ds(1, 3), 0]], axis=1
+            ).reshape(128, chunk)
+            total = dense[:, columns] + dot(pla_v[:, pl.ds(0, 128)], first)
+            total = total + dot(pla_v[:, pl.ds(128, 128)], sib[j].reshape(128, chunk))
             terms[j] = total.astype(BF16).reshape(4, 128, chunk)
-            yield from scatter_x(wire, at, terms.at[j], got.at[j], across.at[j], t + 19, 1.6)
+            yield from scatter_x(wire, at, terms.at[j], got.at[j], across.at[j], (t + 18.6, t + 21.8, t + 23.4))
             total = hid_v[:, columns].astype(F32) + terms[j, 0].astype(F32)
             for n in range(3):
                 total = total + got[j, n].astype(F32)
@@ -691,7 +692,7 @@
             copy.wait_send()
 
     inputs = [table, normed, hidden, placed, in_all, down_all, expert_in, expert_out]
-    copies = 25 + chunks * 18
+    copies = 25 + chunks * 17
     return pl.pallas_call(
         body,
         out_shape=like((128, width)),
@@ -705,11 +706,11 @@
             pltpu.VMEM((2, 3, 16, width), BF16),
             pltpu.VMEM((2, 2, 16, width), BF16),
             pltpu.VMEM((chunks, 3, 4, 2, 16, chunk), BF16),
-            pltpu.VMEM((chunks, 4, 4, 2, 16, chunk), BF16),
-            pltpu.VMEM((chunks, 4, 2, 16, chunk), BF16),
+            *[pltpu.VMEM((chunks, 4, 2, 16, chunk), BF16)] * 4,
+            pltpu.VMEM((chunks, 2, 4, 2, 16, chunk), BF16),
+            pltpu.VMEM((chunks, 2, 2, 16, chunk), BF16),
+            pltpu.VMEM((chunks, 2, 4, 2, 16, chunk), BF16),
             pltpu.VMEM((chunks, 2, 4, 16, chunk), BF16),
-            pltpu.VMEM((chunks, 4, 4, 2, 16, chunk), BF16),
-            pltpu.VMEM((chunks, 4, 4, 16, chunk), BF16),
             pltpu.VMEM((chunks, 4, 128, chunk), BF16),
             pltpu.VMEM((chunks, 3, 128, chunk), BF16),
             pltpu.VMEM((chunks, 2, 64, chunk), BF16),
@@ -760,8 +761,8 @@
     dims = (2, 4, 2)
     sending = named(steps(2, 0, dims) == 1, steps(4, 1, dims), steps(2, 2, dims))
     table = dot(sending, normed).astype(BF16).reshape(2, 4, 2, 16, width)
-    dims = (2, 4, 4)
-    placed = named(steps(4, 1, dims) < 2, steps(4, 2, dims), steps(2, 0, dims)).T
+    dims = (2, 2, 4)
+    placed = named(steps(2, 1, dims) == 0, steps(4, 2, dims), steps(2, 0, dims)).T
     return tail_kernel(
         table, normed, hidden, placed, in_all.reshape(2, width, -1), down_all.reshape(2, width, -1),
         expert_in[0], expert_out[0], 6,

time: 255 us -> 222 us (0.87)
  Pallas kernels: 240 us -> 206 us
    pallas_call x1, Pallas kernels: 147 us -> 120 us  [front_kernel(): pl.pallas_call(body, out_shape=[like(tokens.shape), like((4, *tokens.shap...]
    pallas_call x1, Pallas kernels: 93 us -> 86.6 us  [tail_kernel(): pl.pallas_call(body, out_shape=like((128, width)), in_specs=[pl.BlockSpec...]
where the time goes in v2:
time: 222 us
  Pallas kernels  206 us (93%)
  local copies, waits for them, and re-layouts  7.99 us (4%)
  matrix products  4.19 us (2%)
  other arithmetic  3.62 us (2%)
    pallas_call x1, Pallas kernels, front_kernel(): pl.pallas_call(body, out_shape=[like(tokens.shape), like((4, *tokens.shap...  120 us
    pallas_call x1, Pallas kernels, tail_kernel(): pl.pallas_call(body, out_shape=like((128, width)), in_specs=[pl.BlockSpec...  86.6 us

profile of v2, /device:TPU:1, one launch (start us, length us, event | category | flops | bytes accessed | tf_op | source)
XLA Modules:
  0.0 222.1 jit_solution(17747443959018870368)
XLA Ops:
  0.0 0.9 fusion
  0.9 1.3 bitcast_add_fusion.pos_in
  2.2 0.1 add_multiply_fusion.1
  2.3 0.1 add_multiply_fusion
  2.4 0.1 iota_add_fusion.1
  2.5 0.1 iota_add_fusion
  2.5 1.6 copy.16
  4.1 1.0 copy.15
  5.1 0.9 reshape.119.qkv_in
  6.0 1.8 copy.17
  7.8 119.6 %attention_front.1 = (bf16[128,2048]{1,0:T(8,128)(2,1)}, bf16[4,128,2048]{2,1,0:T(8,128)(2,1)}, s32[4,1,128]{2,1,0:T(1,128)}, bf16[2,2,4,2,2,64,1024]{6,5,4,3,2,...) custom-call(bf16[128,2048]{1,0:T(8,128)(2,1)} %tok.1, s32[1,128]{1,0:T(1,128)} %bitcast_add_fusion.pos_in, ...), custom_call_target="tpu_custom_call" | custom-call | tf_op jit(solution)/shard_map/attention_front/pallas_call | solution.py:469
  127.4 0.8 broadcast_compare_fusion
  128.2 0.8 broadcast_compare_fusion.1
  129.0 0.2 broadcast_and_fusion
  129.2 0.2 and_convert_fusion
  129.4 0.8 copy.18
  130.3 3.3 %convolution_convert_fusion = bf16[256,2048]{1,0:T(8,128)(2,1)} fusion(bf16[512,2048]{1,0:T(8,128)(2,1)} %bitcast.31, pred[32,8,4,128]{3,2,1,0:T(4,128)(4,1)S(1)} %bitcast.42), kind=kOutput, calls=%fused_computation | convolution fusion | flops 537395200 | bytes 3276800 | tf_op jit(solution)/shard_map/dot_general | solution.py:241
  133.6 86.6 %experts_and_dense.1 = bf16[128,2048]{1,0:T(8,128)(2,1)} custom-call(bf16[2,4,2,16,2048]{4,3,2,1,0:T(8,128)(2,1)} %bitcast.37, bf16[512,2048]{1,0:T(8,128)(2,1)} %bitcast.32, bf16[128,2048]{1,0:T(8,128)(2,1)} %get-tuple-element.12.hid, bf16[512,256]{1,0:T(8,128)(2,1)} %bitcast.38, bf16[2,2048,1024]{2,1,0:T(8,128)(2,1)} %bitcast.35, ...), custom_call_target="tpu_custom_call" | custom-call | tf_op jit(solution)/shard_map/experts_and_dense/pallas_call | solution.py:696
  220.2 1.9 copy.28
  (7 shorter events, 0.1 us)

commit v3 on v2

--- a/solution.py
+++ b/solution.py
@@ -181,16 +181,16 @@
         b1 = wire.send(own.at[high], tiles.at[1, high], at.down["x"])
         a2 = wire.send(own.at[high], tiles.at[3, high], at.up["x"])
         b2 = wire.send(own.at[low], tiles.at[1, low], at.down["x"])
-        yield start + block, a1
+        yield start + 1.6 * block, a1
         e = wire.send(tiles.at[3, low], tiles.at[2, low], at.up["x"])
-        yield start + block, b1
+        yield start + 1.6 * block, b1
         f = wire.send(tiles.at[1, high], tiles.at[2, high], at.down["x"])
-        yield start + 2 * block, a2
+        yield start + 2.4 * block, a2
         ready(3)
-        yield start + 2 * block, b2
+        yield start + 2.4 * block, b2
         ready(1)
-        yield start + 3 * block, e
-        yield start + 3 * block, f
+        yield start + 3.3 * block, e
+        yield start + 3.3 * block, f
         ready(2)
     else:
         a = wire.send(own, tiles.at[3], at.up["x"])
@@ -207,16 +207,18 @@
     low, high = pl.ds(0, half), pl.ds(half, half)
     c1 = wire.send(terms.at[2, low], passing.at[0], at.up["x"])
     c2 = wire.send(terms.at[2, high], passing.at[1], at.down["x"])
-    a = wire.send(terms.at[1], got.at[0], at.up["x"])
-    b = wire.send(terms.at[3], got.at[1], at.down["x"])
+    a2 = wire.send(terms.at[1, high], got.at[0, high], at.up["x"])
+    b2 = wire.send(terms.at[3, low], got.at[1, low], at.down["x"])
     yield first, c1
-    d1 = wire.send(passing.at[0], got.at[2, low], at.up["x"])
+    terms[1, low, :] = (terms[1, low, :].astype(F32) + passing[0].astype(F32)).astype(BF16)
+    a1 = wire.send(terms.at[1, low], got.at[0, low], at.up["x"])
     yield first, c2
-    d2 = wire.send(passing.at[1], got.at[2, high], at.down["x"])
-    yield near, a
-    yield near, b
-    yield last, d1
-    yield last, d2
+    terms[3, high, :] = (terms[3, high, :].astype(F32) + passing[1].astype(F32)).astype(BF16)
+    b1 = wire.send(terms.at[3, high], got.at[1, high], at.down["x"])
+    yield near, a2
+    yield near, b2
+    yield last, a1
+    yield last, b1
 
 
 def like(shape, dtype=BF16):
@@ -316,9 +318,9 @@
     def norm(rows, gain):
         return layer_norm(rows, gain[...]).astype(BF16)
 
-    def body(tok, pos_in, qkv_in, out_in, in_in, down_in, gain1, gain2,
+    def body(tok, ids, qkv_in, out_in, in_in, down_in, gain1, gain2,
              hidden, tiles_out, spots, in_all, down_all,
-             tiles, normed, qkv_all, out_all, in_v, down_v, pos_v, keys, theirs, queries,
+             tiles, normed, qkv_all, out_all, in_v, down_v, out_raw, down_raw, ids_v, pos_v, keys, theirs, queries,
              tops, sums, parts, att, terms, got, across, mine, ss, rs, ls):
         at = Spot()
         zh, y, c = at.zh, at.y, at.core
@@ -326,17 +328,18 @@
             (tok, tiles.at[0]),
             (qkv_in.at[0], qkv_all.at[0, zh, y, c, 0]),
             (qkv_in.at[1], qkv_all.at[0, zh, y, c, 1]),
-            (pos_in, pos_v),
-            (out_in.at[0], out_all.at[0, zh, y, c, 0]),
-            (out_in.at[1], out_all.at[0, zh, y, c, 1]),
+            (ids, ids_v),
+            (out_in, out_raw),
+            (down_in, down_raw),
             (in_in, in_v),
-            (down_in, down_v),
         ]
         loads = [pltpu.make_async_copy(src, dst, ls.at[n]) for n, (src, dst) in enumerate(copies)]
         for load in loads:
             load.start()
         greet([at.up["x"], at.down["x"], at.up["y"], at.down["y"], at.up["z"], at.down["z"], at.sibling])
-        for n in (0, 1, 2, 3, 6, 7):
+        for n in (0, 1, 2):
+            loads[n].wait()
+        for n in range(3, 7):
             loads[n].wait()
         copies = [
             (pos_v, spots.at[0]),
@@ -345,41 +348,50 @@
             (down_v.at[0], down_all.at[0, zh, y, c, 0]),
             (down_v.at[1], down_all.at[0, zh, y, c, 1]),
         ]
-        stores = [pltpu.make_async_copy(src, dst, ls.at[8 + n]) for n, (src, dst) in enumerate(copies)]
-        for store in stores:
+        stores = [pltpu.make_async_copy(src, dst, ls.at[10 + n]) for n, (src, dst) in enumerate(copies)]
+        for store in stores[1:3]:
             store.start()
         wire = Wire(ss, rs)
         late, siblings = [], []
 
+        def slots_of_tokens():
+            wanted = jnp.broadcast_to(ids_v[...].astype(F32), (128, 128))
+            order = [lax.broadcasted_iota(jnp.int32, (128, 128), n) for n in range(2)]
+            again = (wanted == wanted.T) & (order[0] < order[1])
+            earlier = jnp.sum(jnp.where(again, 1.0, 0.0), axis=0, keepdims=True)
+            pos_v[...] = ids_v[...] * 4 + earlier.astype(jnp.int32)
+            stores[0].start()
+
         def norm_tile(s):
             normed[pl.ds(s * 128, 128), :] = norm(tiles[s], gain1)
 
         def main():
             yield 1, None
+            out_all[0, zh, y, c] = out_raw[...].T.reshape(2, 64, 256)
+            yield 1.1, None
             norm_tile(0)
-            yield 11.2, None
-            loads[4].wait()
-            loads[5].wait()
+            yield 3.21, None
+            slots_of_tokens()
+            down_v[...] = down_raw[...].T.reshape(2, 64, 1024)
+            for store in stores[3:5]:
+                store.start()
             yield 21, None
             assert len(siblings) == 32
             for copy in siblings:
                 yield 21, copy
-            columns = [pl.ds(h * 384 + 128, 256) for h in range(2)]
             swaps = []
             for r in range(2):
+                part = dot(normed[...], qkv_all[r, :, :, :, :, :, pl.ds(0, 512)].reshape(width, 512)).astype(BF16)
                 for h in range(2):
-                    weight = qkv_all[r, :, :, :, :, :, columns[h]].reshape(width, 256)
-                    keys[r, h] = dot(normed[...], weight).astype(BF16)
+                    keys[r, h] = part[:, h * 256 : (h + 1) * 256]
                     swaps.append(wire.send(keys.at[r, h], theirs.at[1 - r, h], at.pair))
             yield 26, None
-
-            def queries_of(n, carry):
-                column = pl.ds(pl.multiple_of(lax.rem(n, 2) * 384, 128), 128)
-                weight = qkv_all[lax.div(n, 2), :, :, :, :, :, column].reshape(width, 128)
-                queries[n] = dot(normed[...], weight).astype(BF16)
-                return carry
-
-            lax.fori_loop(0, 4, queries_of, 0)
+            both = [
+                dot(normed[...], qkv_all[r, :, :, :, :, :, pl.ds(512, 256)].reshape(width, 256)).astype(BF16)
+                for r in range(2)
+            ]
+            for n in range(4):
+                queries[n] = both[n // 2][:, (n % 2) * 128 : (n % 2 + 1) * 128]
             yield 27, None
 
             def scored(n, rows, pair):
@@ -399,10 +411,10 @@
                     return carry
 
                 lax.fori_loop(0, 4, own_keys, 0)
-                yield 28 + n, None
+                yield 30.7 + n, None
 
             for k, n in enumerate((2, 3, 0, 1)):
-                yield 27 + 5.6 * (k + 1), swaps[k]
+                yield 35 + 5 * k, swaps[k]
 
                 def their_keys(m, carry, n=n):
                     rows = pl.ds(pl.multiple_of(m * 128, 128), 128)
@@ -416,7 +428,7 @@
 
                 lax.fori_loop(0, 4, their_keys, 0)
             for j in range(chunks):
-                late.append(((50 + 0.6 * j, None), mix(j)))
+                late.append(((50.5 + 0.6 * j, None), mix(j)))
 
         left = [chunks]
 
@@ -426,19 +438,19 @@
             second = out_all[1, zhi, pl.ds(yi, 2)].reshape(chunk, 256)
             mixed = dot_nt(att[:, pl.ds(0, 256)], first) + dot_nt(att[:, pl.ds(256, 256)], second)
             terms[j] = mixed.astype(BF16).reshape(4, 128, chunk)
-            yield from scatter_x(wire, at, terms.at[j], got.at[j], across.at[j], (53.4 + 4.2 * j, 56.2 + 4.2 * j, 69.5 + 1.4 * j))
+            yield from scatter_x(wire, at, terms.at[j], got.at[j], across.at[j], (54 + 2.8 * j, 55.4 + 2.8 * j, 66.5 + 1.4 * j))
             columns = pl.ds(j * chunk, chunk)
             total = tiles[0, :, columns].astype(F32) + terms[j, 0].astype(F32)
-            for n in range(3):
+            for n in range(2):
                 total = total + got[j, n].astype(F32)
             hidden[:, columns] = total.astype(BF16)
             left[0] -= 1
             if left[0] == 0:
                 mine[...] = norm(hidden[...], gain2)
-                last = pltpu.make_async_copy(mine, tiles_out.at[0], ls.at[13])
+                last = pltpu.make_async_copy(mine, tiles_out.at[0], ls.at[15])
                 last.start()
                 stores.append(last)
-                stream = gather_x(wire, at, mine, tiles_out, 2, 77, 5.7)
+                stream = gather_x(wire, at, mine, tiles_out, 2, 71, 5.2)
                 late.append((next(stream), stream))
 
         def after(t, stream):
@@ -446,17 +458,17 @@
             yield from stream
 
         run_streams([
-            gather_x(wire, at, pos_v, spots, 1, 30, 20),
+            after(12, gather_x(wire, at, pos_v, spots, 1, 30, 20)),
             gather_x(wire, at, tiles.at[0], tiles, 2, 0, 5.7, norm_tile),
             gather_fine(wire, at, qkv_all, 0, "y", (0, 3.2), late, siblings),
             gather_fine(wire, at, qkv_all, 1, "z", (0, 3.2), late, siblings),
             main(),
-            after(11.3, gather_weight(wire, at, out_all.at[0, zh, y, c, 0], None, out_all, 0, "z", (16.5, 20.9, 21.1, 38, 45))),
-            after(11.3, gather_weight(wire, at, out_all.at[0, zh, y, c, 1], None, out_all, 1, "z", (16.6, 20.9, 21.1, 38, 45))),
-            after(20.95, gather_weight(wire, at, in_v.at[0], stores[1], in_all, 0, "y", (29.5, 31.5, 55.3, 76, 85))),
-            after(20.95, gather_weight(wire, at, in_v.at[1], stores[2], in_all, 1, "y", (29.6, 31.6, 55.4, 80, 90))),
-            after(26.5, gather_weight(wire, at, down_v.at[0], stores[3], down_all, 0, "z", (55.2, 60, 60, 76.5, 85.5))),
-            after(26.6, gather_weight(wire, at, down_v.at[1], stores[4], down_all, 1, "z", (55.2, 60, 60, 80.5, 90.5))),
+            after(11.3, gather_weight(wire, at, out_all.at[0, zh, y, c, 0], None, out_all, 0, "z", (16.5, 20.85, 20.86, 30.8, 40))),
+            after(11.3, gather_weight(wire, at, out_all.at[0, zh, y, c, 1], None, out_all, 1, "z", (16.6, 20.85, 20.86, 30.8, 40))),
+            after(11.4, gather_weight(wire, at, in_v.at[0], stores[1], in_all, 0, "z", (18, 20.92, 31.6, 52.35, 71.5))),
+            after(20.95, gather_weight(wire, at, in_v.at[1], stores[2], in_all, 1, "z", (29.5, 52, 52.1, 64, 79.5))),
+            after(26.5, gather_weight(wire, at, down_v.at[1], stores[4], down_all, 1, "y", (33, 52.4, 52.5, 61.5, 84))),
+            after(26.6, gather_weight(wire, at, down_v.at[0], stores[3], down_all, 0, "y", (33, 52.4, 52.6, 80, 89))),
         ], late)
         for store in [stores[0], *stores[5:]]:
             store.wait()
@@ -473,7 +485,7 @@
             like((4, *tokens.shape)),
             like((4, *pos.shape), jnp.int32),
             like((2, 2, 4, 2, *ffn_in.shape)),
-            like((2, 2, 4, 2, *down.shape)),
+            like((2, 2, 4, 2, 2, 64, down.shape[0])),
         ],
         in_specs=[hbm] * 6 + [vmem] * 2,
         out_specs=[vmem] + [hbm] * 4,
@@ -481,9 +493,12 @@
             pltpu.VMEM((4, *tokens.shape), BF16),
             pltpu.VMEM((512, width), BF16),
             pltpu.VMEM((2, 2, 4, 2, *qkv.shape), BF16),
-            pltpu.VMEM((2, 2, 4, 2, *out.shape), BF16),
+            pltpu.VMEM((2, 2, 4, 2, 2, 64, out.shape[0]), BF16),
             pltpu.VMEM(ffn_in.shape, BF16),
+            pltpu.VMEM((2, 64, down.shape[0]), BF16),
+            pltpu.VMEM(out.shape, BF16),
             pltpu.VMEM(down.shape, BF16),
+            pltpu.VMEM(pos.shape, jnp.int32),
             pltpu.VMEM(pos.shape, jnp.int32),
             pltpu.VMEM((2, 2, 512, 256), BF16),
             pltpu.VMEM((2, 2, 512, 256), BF16),
@@ -493,12 +508,12 @@
             pltpu.VMEM((4, 512, 128), F32),
             pltpu.VMEM((512, 512), BF16),
             pltpu.VMEM((chunks, 4, 128, chunk), BF16),
-            pltpu.VMEM((chunks, 3, 128, chunk), BF16),
+            pltpu.VMEM((chunks, 2, 128, chunk), BF16),
             pltpu.VMEM((chunks, 2, 64, chunk), BF16),
             pltpu.VMEM(tokens.shape, BF16),
             pltpu.SemaphoreType.DMA((copies,)),
             pltpu.SemaphoreType.DMA((copies,)),
-            pltpu.SemaphoreType.DMA((14,)),
+            pltpu.SemaphoreType.DMA((16,)),
         ],
         compiler_params=pltpu.CompilerParams(
             collective_id=number, has_side_effects=True, vmem_limit_bytes=66_000_000
@@ -583,7 +598,7 @@
             return
             yield
 
-        tile = 256
+        tile = 512
 
         def ffn():
             t = 3.0
@@ -595,46 +610,45 @@
                 t += 1.6
 
                 def step(n, carry, part=part):
-                    columns = pl.ds(pl.multiple_of(part * 512 + n * tile, tile), tile)
-                    source = pl.ds(pl.multiple_of((part % 2) * 512 + n * tile, tile), tile)
+                    columns = pl.ds(part * 512, 512)
+                    source = pl.ds((part % 2) * 512, 512)
                     inner = dot(nor_v[...], win_v[part // 2, :, source])
                     units[:, columns] = gelu(inner).astype(BF16)
                     return carry
 
-                lax.fori_loop(0, 2, step, 0)
+                step(0, 0)
             loads[2].wait()
             for part in range(4):
                 yield t, None
                 t += 1.6
 
                 def step(n, carry, part=part):
-                    columns = pl.ds(pl.multiple_of(part * 512 + n * tile, tile), tile)
+                    columns = pl.ds(part * 512, 512)
                     dense[:, columns] = dot_nt(units[:, pl.ds(0, 1024)], wdown_v[0, columns, :]) + dot_nt(
                         units[:, pl.ds(1024, 1024)], wdown_v[1, columns, :]
                     )
                     return carry
 
-                lax.fori_loop(0, 2, step, 0)
+                step(0, 0)
 
         queue = [own_y(), sib_y(), middle(), ffn()]
         run_streams(queue, running)
         own_load.wait()
-        for copy in pair_in:
-            copy.wait_recv()
         loads[3].wait()
 
         def expert_up(first):
             def step(n, carry):
                 columns = pl.ds(pl.multiple_of(n * tile, tile), tile)
-                rows = xx[pl.ds(1 + first, 2)].reshape(256, width)
-                inner = dot(rows, ein_v[:, columns])
-                units[pl.ds(first * 128, 256), columns] = gelu(inner).astype(BF16)
+                rows = jnp.concatenate([xx[first].reshape(128, width), xx[first + 2].reshape(128, width)])
+                inner = gelu(dot(rows, ein_v[:, columns])).astype(BF16)
+                units[pl.ds((first - 1) * 128, 128), columns] = inner[:128]
+                units[pl.ds((first + 1) * 128, 128), columns] = inner[128:]
                 return carry
 
             lax.fori_loop(0, width // tile, step, 0)
 
-        expert_up(0)
-        for copy in far_in:
+        expert_up(1)
+        for copy in pair_in + far_in:
             copy.wait_recv()
         expert_up(2)
         loads[4].wait()
@@ -643,8 +657,8 @@
 
         def one_chunk(j):
             yield 1.5 * j, None
-            for n in range(chunk // tile):
-                inside = pl.ds(n * tile, tile)
+            for n in range(1):
+                inside = pl.ds(0, tile)
                 part = dot(units[...], eout_v[:, pl.ds(j * chunk + n * tile, tile)]).astype(BF16)
                 part = part.reshape(4, 4, 2, 16, tile)
                 mine[j, :, :, :, inside] = part[0]
@@ -681,9 +695,9 @@
             total = dense[:, columns] + dot(pla_v[:, pl.ds(0, 128)], first)
             total = total + dot(pla_v[:, pl.ds(128, 128)], sib[j].reshape(128, chunk))
             terms[j] = total.astype(BF16).reshape(4, 128, chunk)
-            yield from scatter_x(wire, at, terms.at[j], got.at[j], across.at[j], (t + 18.6, t + 21.8, t + 23.4))
+            yield from scatter_x(wire, at, terms.at[j], got.at[j], across.at[j], (t + 19, t + 21, t + 23))
             total = hid_v[:, columns].astype(F32) + terms[j, 0].astype(F32)
-            for n in range(3):
+            for n in range(2):
                 total = total + got[j, n].astype(F32)
             out[:, columns] = total.astype(BF16)
 
@@ -712,7 +726,7 @@
             pltpu.VMEM((chunks, 2, 4, 2, 16, chunk), BF16),
             pltpu.VMEM((chunks, 2, 4, 16, chunk), BF16),
             pltpu.VMEM((chunks, 4, 128, chunk), BF16),
-            pltpu.VMEM((chunks, 3, 128, chunk), BF16),
+            pltpu.VMEM((chunks, 2, 128, chunk), BF16),
             pltpu.VMEM((chunks, 2, 64, chunk), BF16),
             pltpu.SemaphoreType.DMA((copies,)),
             pltpu.SemaphoreType.DMA((copies,)),
@@ -730,18 +744,12 @@
     expert_ids, expert_in, expert_out,
 ):
     count, width = tokens.shape
-    experts, slots = 64, 4
-    chosen = expert_ids[:, 0]
-    one_hot = (chosen[:, None] == jnp.arange(experts, dtype=jnp.int32)[None, :]).astype(BF16)
-    order = jnp.arange(count, dtype=jnp.int32)
-    before = (order[None, :] < order[:, None]).astype(BF16)
-    earlier = jnp.sum(dot(before, one_hot) * one_hot.astype(F32), axis=1)
-    pos = (chosen * slots + earlier.astype(jnp.int32))[None, :]
-
-    qkv_width = qkv_weight.shape[1] * 3 * qkv_weight.shape[3]
+    slots = 4
+    query, pairs = qkv_weight[:, :, 0], qkv_weight[:, :, 1:]
+    qkv = jnp.concatenate([pairs.reshape(128, 512), query.reshape(128, 256)], axis=1).reshape(2, 64, 768)
     hidden, tiles, spots, in_all, down_all = front_kernel(
-        tokens, pos, qkv_weight.reshape(2, -1, qkv_width), out_weight.T.reshape(2, -1, out_weight.shape[0]),
-        ffn_in.reshape(2, -1, ffn_in.shape[1]), ffn_out.T.reshape(2, -1, ffn_out.shape[0]),
+        tokens, expert_ids.reshape(1, count), qkv, out_weight,
+        ffn_in.reshape(2, -1, ffn_in.shape[1]), ffn_out,
         ln1_gain[None, :], ln2_gain[None, :], 1,
     )
     normed = tiles.reshape(4 * count, width)

time: 222 us -> 210 us (0.946)
  Pallas kernels: 206 us -> 198 us
  local copies, waits for them, and re-layouts: 7.99 us -> 4.86 us
    pallas_call x1, Pallas kernels: 120 us -> 114 us  [front_kernel(): pl.pallas_call(body, out_shape=[like(tokens.shape), like((4, *tokens.shap...]
    transpose x2 -> x0, local copies, waits for them, and re-layouts: 3.36 us -> none  [the longest x1 1.79 us: shards(): ffn_out.T.reshape(2, -1, ffn_out.shape[0])]
where the time goes in v3:
time: 210 us
  Pallas kernels  198 us (94%)
  local copies, waits for them, and re-layouts  4.86 us (2%)
  matrix products  3.31 us (2%)
  other arithmetic  3.05 us (1%)
    pallas_call x1, Pallas kernels, front_kernel(): pl.pallas_call(body, out_shape=[like(tokens.shape), like((4, *tokens.shap...  114 us
    pallas_call x1, Pallas kernels, tail_kernel(): pl.pallas_call(body, out_shape=like((128, width)), in_specs=[pl.BlockSpec...  84.8 us

profile of v3, /device:TPU:1, one launch (start us, length us, event | category | flops | bytes accessed | tf_op | source)
XLA Modules:
  0.0 209.7 jit_solution(1990083068898571335)
XLA Ops:
  0.1 0.1 add_multiply_fusion.1
  0.2 0.1 add_multiply_fusion
  0.2 0.1 iota_add_fusion.1
  0.3 0.1 iota_add_fusion
  0.4 0.9 slice.7
  1.3 1.0 slice.6
  2.4 0.1 copy.13
  2.5 0.1 concatenate.8
  2.5 0.7 pad_maximum_fusion.qkv_in
  3.2 113.6 %attention_front.1 = (bf16[128,2048]{1,0:T(8,128)(2,1)}, bf16[4,128,2048]{2,1,0:T(8,128)(2,1)}, s32[4,1,128]{2,1,0:T(1,128)}, bf16[2,2,4,2,2,64,1024]{6,5,4,3,2,...) custom-call(bf16[128,2048]{1,0:T(8,128)(2,1)} %tok.1, s32[1,128]{1,0:T(1,128)} %bitcast.41, ...), custom_call_target="tpu_custom_call" | custom-call | tf_op jit(solution)/shard_map/attention_front/pallas_call | solution.py:481
  116.8 0.8 broadcast_compare_fusion
  117.6 0.8 broadcast_compare_fusion.1
  118.4 0.2 broadcast_and_fusion
  118.6 0.2 and_convert_fusion
  118.8 0.8 copy.14
  119.7 3.3 %convolution_convert_fusion = bf16[256,2048]{1,0:T(8,128)(2,1)} fusion(bf16[512,2048]{1,0:T(8,128)(2,1)} %bitcast.25, pred[32,8,4,128]{3,2,1,0:T(4,128)(4,1)S(1)} %bitcast.35), kind=kOutput, calls=%fused_computation | convolution fusion | flops 537395200 | bytes 3276800 | tf_op jit(solution)/shard_map/dot_general | solution.py:243
  123.0 84.8 %experts_and_dense.1 = bf16[128,2048]{1,0:T(8,128)(2,1)} custom-call(bf16[2,4,2,16,2048]{4,3,2,1,0:T(8,128)(2,1)} %bitcast.31, bf16[512,2048]{1,0:T(8,128)(2,1)} %bitcast.26, bf16[128,2048]{1,0:T(8,128)(2,1)} %get-tuple-element.12.hid, bf16[512,256]{1,0:T(8,128)(2,1)} %bitcast.32, bf16[2,2048,1024]{2,1,0:T(8,128)(2,1)} %bitcast.29, ...), custom_call_target="tpu_custom_call" | custom-call | tf_op jit(solution)/shard_map/experts_and_dense/pallas_call | solution.py:710
  207.8 1.9 copy.24
  (8 shorter events, 0.2 us)

commit v4 on v3

--- a/solution.py
+++ b/solution.py
@@ -522,23 +522,42 @@
     )(*inputs)
 
 
-def tail_kernel(table, normed, hidden, placed, in_all, down_all, expert_in, expert_out, number):
+def tail_kernel(spots, normed, hidden, in_all, down_all, expert_in, expert_out, number):
     width = normed.shape[1]
     chunk, chunks = 512, width // 512
 
-    def body(tab, nor, hid, pla, win, wdown, ein, eout, out,
-             nor_v, hid_v, pla_v, win_v, wdown_v, ein_v, eout_v,
+    def body(spo, nor, hid, win, wdown, ein, eout, out,
+             spo_v, tab, pla_v, nor_v, hid_v, win_v, wdown_v, ein_v, eout_v,
              units, dense, xx, aside, passing, away, mine, hop, other, summed, both_sums, near, ahead, sib,
              terms, got, across, ss, rs, ls):
         at = Spot()
         cross = {"zh": 1 - at.zh, "zl": 1 - at.zl}
-        own_load = pltpu.make_async_copy(tab.at[:, 0, 0], xx.at[pl.ds(0, 2), 0, 0], ls.at[0])
-        pairs = [(nor, nor_v), (win, win_v), (wdown, wdown_v), (ein, ein_v), (eout, eout_v), (pla, pla_v), (hid, hid_v)]
+        own_load = pltpu.make_async_copy(spo, spo_v, ls.at[0])
+        pairs = [(nor, nor_v), (win, win_v), (wdown, wdown_v), (ein, ein_v), (eout, eout_v), (hid, hid_v)]
         loads = [pltpu.make_async_copy(src, dst, ls.at[1 + n]) for n, (src, dst) in enumerate(pairs)]
         own_load.start()
         for load in loads:
             load.start()
         greet([at.up["x"], at.down["x"], at.up["y"], at.down["y"], at.sibling, at.pair, cross])
+        own_load.wait()
+        tokens_at = jnp.concatenate([spo_v[n] for n in range(4)], axis=1)
+        dims = (256, 512)
+        line = lax.broadcasted_iota(jnp.int32, dims, 0)
+        source = lax.broadcasted_iota(jnp.int32, dims, 1) >> 7
+
+        def named(pair, dy, dc):
+            zh = jnp.where(pair, at.zh, 1 - at.zh)
+            expert = ((zh * 4 + ((at.y + dy) & 3)) * 2 + ((at.core + dc) & 1)) * 4 + at.x
+            hit = (expert * 4 + (line & 3) == tokens_at) & (((line >> 2) & 3) == source)
+            return jnp.where(hit, 1.0, 0.0)
+
+        sending = named((line >> 7) == 1, (line >> 5) & 3, (line >> 4) & 1).astype(BF16)
+        loads[0].wait()
+        for n in range(width // 512):
+            columns = pl.ds(n * 512, 512)
+            rows = dot(sending, nor_v[:, columns]).astype(BF16).reshape(2, 4, 2, 16, 512)
+            tab[:, :, :, :, columns] = rows
+            xx[pl.ds(0, 2), 0, 0, :, columns] = rows[:, 0, 0]
         wire = Wire(ss, rs)
         both = pl.ds(0, 2)
         core0 = wire.send(tab.at[:, 0, 1], xx.at[both, 0, 1], at.sibling)
@@ -603,7 +622,8 @@
         def ffn():
             t = 3.0
             yield t, None
-            loads[0].wait()
+            placed = named(((line >> 6) & 1) == 0, (line >> 4) & 3, line >> 7)
+            pla_v[...] = placed.T.astype(BF16)
             loads[1].wait()
             for part in range(4):
                 yield t, None
@@ -633,7 +653,6 @@
 
         queue = [own_y(), sib_y(), middle(), ffn()]
         run_streams(queue, running)
-        own_load.wait()
         loads[3].wait()
 
         def expert_up(first):
@@ -653,7 +672,6 @@
         expert_up(2)
         loads[4].wait()
         loads[5].wait()
-        loads[6].wait()
 
         def one_chunk(j):
             yield 1.5 * j, None
@@ -705,7 +723,7 @@
         for copy in wire.sent:
             copy.wait_send()
 
-    inputs = [table, normed, hidden, placed, in_all, down_all, expert_in, expert_out]
+    inputs = [spots, normed, hidden, in_all, down_all, expert_in, expert_out]
     copies = 25 + chunks * 17
     return pl.pallas_call(
         body,
@@ -713,7 +731,10 @@
         in_specs=[pl.BlockSpec(memory_space=pl.ANY)] * len(inputs),
         out_specs=pl.BlockSpec(memory_space=pltpu.VMEM),
         scratch_shapes=[
-            *[pltpu.VMEM(a.shape, BF16) for a in (normed, hidden, placed, in_all, down_all, expert_in, expert_out)],
+            pltpu.VMEM(spots.shape, jnp.int32),
+            pltpu.VMEM((2, 4, 2, 16, width), BF16),
+            pltpu.VMEM((512, 256), BF16),
+            *[pltpu.VMEM(a.shape, BF16) for a in (normed, hidden, in_all, down_all, expert_in, expert_out)],
             pltpu.VMEM((512, width), BF16),
             pltpu.VMEM((512, width), F32),
             pltpu.VMEM((5, 4, 2, 16, width), BF16),
@@ -744,7 +765,6 @@
     expert_ids, expert_in, expert_out,
 ):
     count, width = tokens.shape
-    slots = 4
     query, pairs = qkv_weight[:, :, 0], qkv_weight[:, :, 1:]
     qkv = jnp.concatenate([pairs.reshape(128, 512), query.reshape(128, 256)], axis=1).reshape(2, 64, 768)
     hidden, tiles, spots, in_all, down_all = front_kernel(
@@ -754,25 +774,8 @@
     )
     normed = tiles.reshape(4 * count, width)
 
-    zh, y, core, x = (lax.axis_index(name) for name in ("zh", "y", "core", "x"))
-
-    def named(pair, dy, dc):
-        expert = (((jnp.where(pair, zh, 1 - zh) * 4 + (y + dy) % 4) * 2 + (core + dc) % 2) * 4) + x
-        wanted = expert[..., None] * slots + jnp.arange(slots, dtype=jnp.int32)
-        hit = wanted[..., None, :, None, None] == spots.reshape(4, count)
-        same = jnp.arange(4)[:, None, None, None] == jnp.arange(4)[None, None, :, None]
-        return (hit & same).astype(BF16).reshape(-1, 4 * count)
-
-    def steps(size, dim, dims):
-        return lax.broadcasted_iota(jnp.int32, dims, dim)
-
-    dims = (2, 4, 2)
-    sending = named(steps(2, 0, dims) == 1, steps(4, 1, dims), steps(2, 2, dims))
-    table = dot(sending, normed).astype(BF16).reshape(2, 4, 2, 16, width)
-    dims = (2, 2, 4)
-    placed = named(steps(2, 1, dims) == 0, steps(4, 2, dims), steps(2, 0, dims)).T
     return tail_kernel(
-        table, normed, hidden, placed, in_all.reshape(2, width, -1), down_all.reshape(2, width, -1),
+        spots, normed, hidden, in_all.reshape(2, width, -1), down_all.reshape(2, width, -1),
         expert_in[0], expert_out[0], 6,
     )
 

time: 210 us -> 204 us (0.971)
  matrix products: 3.31 us -> 0 us
  other arithmetic: 3.05 us -> 0.69 us
    dot_general x1 -> x0, matrix products: 3.31 us -> none  [dot(): return jnp.dot(a, b, preferred_element_type=F32)]
where the time goes in v4:
time: 204 us
  Pallas kernels  199 us (98%)
  local copies, waits for them, and re-layouts  3.97 us (2%)
    pallas_call x1, Pallas kernels, front_kernel(): pl.pallas_call(body, out_shape=[like(tokens.shape), like((4, *tokens.shap...  114 us
    pallas_call x1, Pallas kernels, tail_kernel(): pl.pallas_call(body, out_shape=like((128, width)), in_specs=[pl.BlockSpec...  85.9 us

profile of v4, /device:TPU:1, one launch (start us, length us, event | category | flops | bytes accessed | tf_op | source)
XLA Modules:
  0.0 204.2 jit_solution(16237783235869210280)
XLA Ops:
  0.0 0.9 slice.7
  0.9 1.0 slice.6
  1.9 0.1 copy.11
  2.0 0.1 concatenate.8
  2.1 0.7 pad_maximum_fusion.qkv_in
  2.8 113.6 %attention_front.1 = (bf16[128,2048]{1,0:T(8,128)(2,1)}, bf16[4,128,2048]{2,1,0:T(8,128)(2,1)}, s32[4,1,128]{2,1,0:T(1,128)}, bf16[2,2,4,2,2,64,1024]{6,5,4,3,2,...) custom-call(bf16[128,2048]{1,0:T(8,128)(2,1)} %tok.1, s32[1,128]{1,0:T(1,128)} %bitcast.19, ...), custom_call_target="tpu_custom_call" | custom-call | tf_op jit(solution)/shard_map/attention_front/pallas_call | solution.py:481
  116.4 85.9 %experts_and_dense.1 = bf16[128,2048]{1,0:T(8,128)(2,1)} custom-call(s32[4,1,128]{2,1,0:T(1,128)} %get-tuple-element.10.spo, bf16[512,2048]{1,0:T(8,128)(2,1)} %bitcast.15, bf16[128,2048]{1,0:T(8,128)(2,1)} %get-tuple-element.12.hid, bf16[2,2048,1024]{2,1,0:T(8,128)(2,1)} %bitcast.13, bf16[2,2048,1024]{2,1,0:T(8,128)(2,1)} %bitcast.14, ...), custom_call_target="tpu_custom_call" | custom-call | tf_op jit(solution)/shard_map/experts_and_dense/pallas_call | solution.py:728
  202.3 1.9 copy.13
  (1 shorter events, 0.0 us)
